TPU v7x, 1024 devices: a whole 4x4x32 slice. The times are simulated.
1024 devices in a mesh: gx: 4 (over z_hi, core), gy: 16 (over z_lo), gz: 16 (over y, x).
Axes of the slice: x: 4, y: 4, z: 32 (z_hi: 2, z_lo: 16; z = z_hi * 16 + z_lo), core: 2. Of those that a mesh axis runs over, the one named last changes fastest.
Arguments:
- positions: float32 [4, 16, 16, 2, 3, 128], P('gx', 'gy', 'gz'), may hold values from 0 to 48, as said below
- features: bfloat16 [4, 16, 16, 2, 128, 128], P('gx', 'gy', 'gz'), may hold values from -6 to 6
- counts: int32 [4, 16, 16, 2], P('gx', 'gy', 'gz'), may hold values from 0 to 128, as said below
- neighbours: int32 [4, 16, 16, 2, 8], P('gx', 'gy', 'gz'), may hold values from -1 to 53, as said below
- mix_weight: bfloat16 [1024, 128], replicated, may hold values from -0.1875 to 0.1875
- readout: float32 [128], replicated, may hold values from -4 to 4
- radial_rates: float32 [4], replicated, may hold values from 0.03 to 0.6
Outputs:
- forces: float32 [4, 16, 16, 2, 3, 128], P('gx', 'gy', 'gz')
- feature_grads: float32 [4, 16, 16, 2, 128, 128], P('gx', 'gy', 'gz')
Inputs may be any that keep to these rules, and one draw needn't show every extreme that they name: The atoms of a tile fill its first counts slots; a count of 0 marks a tile slot that its device doesn't own; every draw has a tile with 128 atoms. neighbours[.., t, s] names a tile of the device's neighbourhood as ((dx + 1) * 9 + (dy + 1) * 3 + (dz + 1)) * 2 + u, dx, dy, dz in -1..1 being the device offsets along gx, gy, gz and u the tile slot; slot 0 names tile t itself, every other used slot names a tile with one or more atoms, the entries of a row differ, and -1 marks unused slots, which come after the used ones. `positions`: the atoms of device (a, b, c) lie in the cube of side 3 whose lowest corner is 3 (a, b, c).
All inputs are finite; a program needn't handle non-finite values.
Results may differ from a plain program's by a relative error of at most 0.0008.
Values may be sent and summed in bfloat16 or wider, within the bound.
A program may use at most 32 MiB of HBM per device.

v0:
```python
import jax
import jax.numpy as jnp
from jax import lax
from jax.sharding import PartitionSpec as P


def extended(block, sides, width):
    for axis, dim in sides:
        count = lax.axis_size(axis)
        forward = [(i, i + 1) for i in range(count - 1)]
        backward = [(target, source) for source, target in forward]
        low = lax.ppermute(
            lax.slice_in_dim(block, block.shape[dim] - width, None, axis=dim), axis, forward
        )
        high = lax.ppermute(lax.slice_in_dim(block, 0, width, axis=dim), axis, backward)
        block = jnp.concatenate([low, block, high], axis=dim)
    return block


def from_behind(block, axis, distance):
    devices = range(lax.axis_size(axis))
    route = [(i - distance, i) for i in devices if i - distance in devices]
    return lax.ppermute(block, axis, route)


def build_basis(own_points, other_points, decay_rates):
    offset = other_points[None, :, :] - jnp.transpose(own_points)[:, :, None]
    square_dist = jnp.sum(offset * offset, axis=1)
    radial = jnp.exp(-decay_rates[None, :, None] * square_dist[:, None, :])
    pair_basis = jnp.concatenate(
        [radial[:, :, None, :], radial[:, :, None, :] * offset[:, None, :, :]], axis=2
    )
    return (offset, radial, pair_basis)


def device_terms(
    own_points,
    own_valid,
    own_counts,
    near_points,
    near_features,
    neighbour_rows,
    mixing,
    readout,
    decay_rates,
):
    tile_count = own_points.shape[0]
    atom_count = own_points.shape[2]
    channel_count = near_features.shape[2]
    slot_count = neighbour_rows.shape[1]
    radial_count = decay_rates.shape[0]
    basis_count = 4 * radial_count
    scaling = (slot_count * atom_count) ** (-0.5)
    pair_count = tile_count * slot_count
    row_width = (3 + channel_count) * atom_count

    def locate(pair_index):
        tile_index = pair_index // slot_count
        slot_index = pair_index % slot_count
        target = neighbour_rows[tile_index, slot_index]
        is_live = target >= 0
        source_index = jnp.maximum(target, 0)
        active = is_live & (own_counts[tile_index] > 0)
        return (tile_index, source_index, is_live, active)

    def forward_pair(pair_index, summed):
        tile_index, source_index, is_live, active = locate(pair_index)
        near_tile = jnp.where(is_live, near_features[source_index], jnp.zeros((), jnp.bfloat16))
        offset, radial, pair_basis = build_basis(
            own_points[tile_index], near_points[source_index], decay_rates
        )
        flat_basis = pair_basis.reshape(atom_count * basis_count, atom_count).astype(jnp.bfloat16)
        contribution = jnp.dot(flat_basis, near_tile, preferred_element_type=jnp.float32)
        return lax.dynamic_update_index_in_dim(
            summed, summed[tile_index] + contribution, tile_index, 0
        )

    summed = lax.fori_loop(
        0,
        pair_count,
        forward_pair,
        jnp.zeros((tile_count, atom_count * basis_count, channel_count), jnp.float32),
    )
    scaled_sum = summed.reshape(tile_count, atom_count, radial_count, 4, channel_count) * scaling
    scalar_part = scaled_sum[:, :, :, 0, :]
    vector_norm = jnp.sum(scaled_sum[:, :, :, 1:, :] * scaled_sum[:, :, :, 1:, :], axis=3)
    invariant = (
        jnp.concatenate([scalar_part, vector_norm], axis=2)
        .reshape(tile_count * atom_count, 2 * radial_count * channel_count)
        .astype(jnp.bfloat16)
    )
    preact = jnp.dot(invariant, mixing, preferred_element_type=jnp.float32)
    sigmoid_value = jax.nn.sigmoid(preact)
    grad_pre = (
        own_valid.reshape(-1, 1)
        * readout[None, :]
        * sigmoid_value
        * (1.0 + preact * (1.0 - sigmoid_value))
    ).astype(jnp.bfloat16)
    grad_invariant = lax.dot_general(
        grad_pre, mixing, (((1,), (1,)), ((), ())), preferred_element_type=jnp.float32
    )
    grad_invariant = grad_invariant.reshape(tile_count, atom_count, 2, radial_count, channel_count)
    grad_sum = (
        jnp.concatenate(
            [
                grad_invariant[:, :, 0, :, None, :],
                2.0 * scaled_sum[:, :, :, 1:, :] * grad_invariant[:, :, 1, :, None, :],
            ],
            axis=3,
        )
        * scaling
    )
    grad_sum = grad_sum.reshape(tile_count, atom_count * basis_count, channel_count).astype(
        jnp.bfloat16
    )

    def backward_pair(pair_index, state_pair):
        own_force, ghost_sum = state_pair
        tile_index, source_index, is_live, active = locate(pair_index)
        near_tile = jnp.where(is_live, near_features[source_index], jnp.zeros((), jnp.bfloat16))
        offset, radial, pair_basis = build_basis(
            own_points[tile_index], near_points[source_index], decay_rates
        )
        flat_basis = pair_basis.reshape(atom_count * basis_count, atom_count).astype(jnp.bfloat16)
        seed_rows = grad_sum[tile_index]
        grad_basis = lax.dot_general(
            seed_rows, near_tile, (((1,), (1,)), ((), ())), preferred_element_type=jnp.float32
        )
        grad_basis = grad_basis.reshape(atom_count, radial_count, 4, atom_count)
        grad_near = lax.dot_general(
            flat_basis, seed_rows, (((0,), (0,)), ((), ())), preferred_element_type=jnp.float32
        )
        inner_term = grad_basis[:, :, 0, :] + jnp.sum(
            grad_basis[:, :, 1:, :] * offset[:, None, :, :], axis=2
        )
        pair_force = jnp.sum(
            radial[:, :, None, :]
            * (
                grad_basis[:, :, 1:, :]
                - 2.0
                * decay_rates[None, :, None, None]
                * offset[:, None, :, :]
                * inner_term[:, :, None, :]
            ),
            axis=1,
        )
        own_part = jnp.transpose(jnp.sum(pair_force, axis=2))
        ghost_part = jnp.concatenate(
            [-jnp.sum(pair_force, axis=0).reshape(-1), grad_near.reshape(-1)]
        ) * is_live.astype(jnp.float32)
        own_part, ghost_part = (own_part, ghost_part)
        own_force = lax.dynamic_update_index_in_dim(
            own_force, own_force[tile_index] + own_part, tile_index, 0
        )
        ghost_sum = lax.dynamic_update_index_in_dim(
            ghost_sum, ghost_sum[source_index] + ghost_part, source_index, 0
        )
        return (own_force, ghost_sum)

    start_pair = (
        jnp.zeros((tile_count, 3, atom_count), jnp.float32),
        jnp.zeros((27 * tile_count, row_width), jnp.float32),
    )
    return lax.fori_loop(0, pair_count, backward_pair, start_pair)


def fold_plane(buffer, axis_dim, sender):
    lower_plane = lax.slice_in_dim(buffer, 0, 1, axis=axis_dim)
    middle_plane = lax.slice_in_dim(buffer, 1, 2, axis=axis_dim)
    upper_plane = lax.slice_in_dim(buffer, 2, 3, axis=axis_dim)
    result = middle_plane
    for toward in (1, -1):
        result = result + sender(upper_plane if toward == 1 else lower_plane, toward)
    return result


def body(positions, features, counts, neighbours, mix_weight, readout, radial_rates):
    tile_count = positions.shape[3]
    atom_count = positions.shape[5]
    channel_count = features.shape[5]
    row_width = (3 + channel_count) * atom_count
    own_counts = counts.reshape(tile_count)
    is_valid = lax.broadcasted_iota(jnp.int32, (tile_count, atom_count), 1) < own_counts[:, None]
    valid_float = is_valid.astype(jnp.float32)
    masked = jnp.where(
        is_valid.reshape(1, 1, 1, tile_count, atom_count, 1), features, jnp.zeros((), jnp.bfloat16)
    )
    near_points = extended(positions, (("gx", 0), ("gy", 1), ("gz", 2)), 1)
    near_features = extended(masked, (("gx", 0), ("gy", 1), ("gz", 2)), 1)
    near_points = near_points.reshape(27 * tile_count, 3, atom_count)
    near_features = near_features.reshape(27 * tile_count, atom_count, channel_count)
    own_force, ghost_sum = device_terms(
        positions.reshape(tile_count, 3, atom_count),
        valid_float,
        own_counts,
        near_points,
        near_features,
        neighbours.reshape(tile_count, -1),
        mix_weight,
        readout,
        radial_rates,
    )
    buffer = ghost_sum.reshape(3, 3, 3, tile_count, row_width)
    buffer = fold_plane(buffer, 2, lambda values, toward: from_behind(values, "gz", toward))
    buffer = fold_plane(buffer, 1, lambda values, toward: from_behind(values, "gy", toward))
    buffer = fold_plane(buffer, 0, lambda values, toward: from_behind(values, "gx", toward))
    center = buffer.reshape(tile_count, row_width)
    forces = own_force + center[:, : 3 * atom_count].reshape(tile_count, 3, atom_count)
    feature_grads = (
        center[:, 3 * atom_count :].reshape(tile_count, atom_count, channel_count)
        * valid_float[:, :, None]
    )
    return (
        forces.reshape(1, 1, 1, tile_count, 3, atom_count),
        feature_grads.reshape(1, 1, 1, tile_count, atom_count, channel_count),
    )


def solution(mesh):
    in_specs = (
        P("gx", "gy", "gz", None, None, None),
        P("gx", "gy", "gz", None, None, None),
        P("gx", "gy", "gz", None),
        P("gx", "gy", "gz", None, None),
        P(),
        P(),
        P(),
    )
    out_specs = (P("gx", "gy", "gz", None, None, None), P("gx", "gy", "gz", None, None, None))
    return jax.shard_map(body, mesh=mesh, in_specs=in_specs, out_specs=out_specs, check_vma=False)
```

profile of v0, /device:TPU:25, one launch (start us, length us, event | category | flops | bytes accessed | tf_op | source)
XLA Modules:
  0.0 422.3 jit_solution(15274461035101302283)
XLA Ops:
  2.4 2.6 collective-permute-start.7
  5.0 28.6 %collective-permute-start.6 = (bf16[1,1,1,2,128,128]{5,4,3,2,1,0:T(8,128)(2,1)S(1)}, bf16[1,1,1,2,128,128]{5,4,3,2,1,0:T(8,128)(2,1)S(1)}, u32[]{:S(2)}, u32[]{:S(2)}) collective-permute-start(bf16[1,1,1,2,128,128]{5,4,3,2,1,0:T(8,128)(2,1)S(1)} %broadcast_select_fusion), channel_id=1, source_target_pairs={{0,256},{256,512},{512,768},{1,257},{257,513},{513,769},{2,258},{2... | collective-permute-start | bytes 196616 | tf_op jit(solution)/shard_map/ppermute | solution.py:12
  36.2 4.0 collective-permute-start.8
  40.2 23.3 %collective-permute-start = (f32[1,1,1,2,3,128]{5,3,4,2,1,0:T(2,128)}, f32[1,1,1,2,3,128]{5,3,4,2,1,0:T(2,128)S(1)}, u32[]{:S(2)}, u32[]{:S(2)}) collective-permute-start(f32[1,1,1,2,3,128]{5,3,4,2,1,0:T(2,128)} %param.11), channel_id=1, source_target_pairs={{0,256},{256,512},{512,768},{1,257},{257,513},{513,769},{2,258},{2... | collective-permute-start | bytes 9224 | tf_op jit(solution)/shard_map/ppermute | solution.py:12
  63.5 1.9 collective-permute-start.1
  65.6 4.6 %collective-permute-start.11 = (bf16[3,3,1,2,128,128]{5,4,3,2,1,0:T(8,128)(2,1)S(1)}, bf16[3,3,1,2,128,128]{5,4,3,2,1,0:T(8,128)(2,1)S(1)}, u32[]{:S(2)}, u32[]{:S(2)}) collective-permute-start(bf16[3,3,1,2,128,128]{5,4,3,2,1,0:T(8,128)(2,1)S(1)} %pad_maximum_fusion.3), channel_id=1, source_target_pairs={{1,0},{2,1},{3,2},{4,3},{5,4},{6,5},{7,6},{8,7},{9,8},{10,9},{11,1... | collective-permute-start | bytes 1769480 | tf_op jit(solution)/shard_map/ppermute | solution.py:15
  70.1 1.9 collective-permute-start.10
  72.8 14.2 %collective-permute-done.1 = f32[1,1,1,2,3,128]{5,3,4,2,1,0:T(2,128)S(1)} collective-permute-done((f32[1,1,1,2,3,128]{5,3,4,2,1,0:T(2,128)}, f32[1,1,1,2,3,128]{5,3,4,2,1,0:T(2,128)S(1)}, u32[]{:S(2)}, u32[]{:S(2)}) %collective-permute-start.1) | collective-permute-done | bytes 3104 | tf_op jit(solution)/shard_map/ppermute | solution.py:15
  88.3 4.0 collective-permute-start.2
  93.1 4.6 %collective-permute-start.5 = (f32[3,3,1,2,3,128]{5,3,4,2,1,0:T(2,128)S(1)}, f32[3,3,1,2,3,128]{5,3,4,2,1,0:T(2,128)S(1)}, u32[]{:S(2)}, u32[]{:S(2)}) collective-permute-start(f32[3,3,1,2,3,128]{5,3,4,2,1,0:T(2,128)S(1)} %pad_maximum_fusion.7), channel_id=1, source_target_pairs={{1,0},{2,1},{3,2},{4,3},{5,4},{6,5},{7,6},{8,7},{9,8},{10,9},{11,1... | collective-permute-start | bytes 82952 | tf_op jit(solution)/shard_map/ppermute | solution.py:15
  97.6 1.9 collective-permute-start.4
  100.9 3.4 collective-permute-done.4
  104.5 1.4 pad_maximum_fusion.2
  106.0 77.2 %while.32 = (s32[]{:T(128)}, f32[2,2048,128]{2,1,0:T(8,128)S(1)}, f32[1,4,1]{1,2,0:T(1,128)S(1)}, s32[2,8]{1,0:T(2,128)S(1)}, f32[54,3,128]{2,1,0:T(4,128)S(1)},...) while((s32[]{:T(128)}, f32[2,2048,128]{2,1,0:T(8,128)S(1)}, ...), condition=%wide.region_2.3_spmd, body=%wide.region_0.2_spmd.sunk | while | flops 69156888 | bytes 8104349 | solution.py:78
  183.4 1.7 multiply_reduce_fusion.3
  186.0 1.5 fusion.38
  187.5 1.8 reshape.285
  191.5 2.1 broadcast_in_dim.102
  193.5 136.3 %while.33 = (s32[]{:T(128)}, f32[2,3,128]{2,0,1:T(2,128)S(1)}, f32[54,16768]{1,0:T(8,128)}, f32[1,4,1]{1,2,0:T(1,128)S(1)}, s32[2,8]{1,0:T(2,128)S(1)}, /*index=...) while((s32[]{:T(128)}, f32[2,3,128]{2,0,1:T(2,128)S(1)}, ...), condition=%wide.region_9.10_spmd, body=%wide.region_4.9_spmd.sunk | while | flops 136840352 | bytes 10953210 | solution.py:165
  199.5 2.6 dynamic_update_slice.39
  208.0 2.6 dynamic_update_slice.39
  216.5 2.6 dynamic_update_slice.39
  225.0 2.6 dynamic_update_slice.39
  233.5 2.6 dynamic_update_slice.39
  242.0 2.6 dynamic_update_slice.39
  250.6 2.6 dynamic_update_slice.39
  259.1 2.6 dynamic_update_slice.39
  267.6 2.6 dynamic_update_slice.39
  276.1 2.6 dynamic_update_slice.39
  284.6 2.6 dynamic_update_slice.39
  293.1 2.6 dynamic_update_slice.39
  301.7 2.6 dynamic_update_slice.39
  310.2 2.6 dynamic_update_slice.39
  318.7 2.6 dynamic_update_slice.39
  327.2 2.6 dynamic_update_slice.39
  329.8 5.4 %reshape.286 = f32[3,3,3,2,16768]{4,3,2,1,0:T(2,128)} reshape(f32[54,16768]{1,0:T(8,128)} %get-tuple-element.415) | data formatting | bytes 7243776 | tf_op jit(solution)/shard_map/reshape | solution.py:204
  335.2 1.8 fusion.48
  337.0 1.9 collective-permute-start.12
  338.9 5.5 %collective-permute-start.13 = (f32[3,3,1,2,16768]{4,3,2,1,0:T(2,128)S(1)}, f32[3,3,1,2,16768]{4,3,2,1,0:T(2,128)S(1)}, u32[]{:S(2)}, u32[]{:S(2)}) collective-permute-start(f32[3,3,1,2,16768]{4,3,2,1,0:T(2,128)S(1)} %get-tuple-element.462), channel_id=1, source_target_pairs={{1,0},{2,1},{3,2},{4,3},{5,4},{6,5},{7,6},{8,7},{9,8},{10,9},{11,1... | collective-permute-start | bytes 3621896 | tf_op jit(solution)/shard_map/ppermute | solution.py:23
  344.4 11.9 %collective-permute-done.12 = f32[3,3,1,2,16768]{4,3,2,1,0:T(2,128)S(1)} collective-permute-done((f32[3,3,1,2,16768]{4,3,2,1,0:T(2,128)S(1)}, f32[3,3,1,2,16768]{4,3,2,1,0:T(2,128)S(1)}, u32[]{:S(2)}, u32[]{:S(2)}) %collective-permute-start.12) | collective-permute-done | bytes 1207328 | tf_op jit(solution)/shard_map/ppermute | solution.py:23
  356.3 1.5 collective-permute-done.13
  357.8 2.1 fusion.27
  360.0 3.6 collective-permute-start.14
  365.0 3.5 collective-permute-done.14
  368.4 3.8 collective-permute-done.15
  372.6 14.6 %collective-permute-start.16 = (f32[1,1,1,2,16768]{4,3,2,1,0:T(2,128)S(1)}, f32[1,1,1,2,16768]{4,3,2,1,0:T(2,128)S(1)}, u32[]{:S(2)}, u32[]{:S(2)}) collective-permute-start(f32[1,1,1,2,16768]{4,3,2,1,0:T(2,128)S(1)} %get-tuple-element.467), channel_id=1, source_target_pairs={{0,256},{256,512},{512,768},{1,257},{257,513},{513,769},{2,258},{2... | collective-permute-start | bytes 402440 | tf_op jit(solution)/shard_map/ppermute | solution.py:23
  387.2 1.9 collective-permute-start.17
  389.2 31.6 %collective-permute-done.17 = f32[1,1,1,2,16768]{4,3,2,1,0:T(2,128)S(1)} collective-permute-done((f32[1,1,1,2,16768]{4,3,2,1,0:T(2,128)S(1)}, f32[1,1,1,2,16768]{4,3,2,1,0:T(2,128)S(1)}, u32[]{:S(2)}, u32[]{:S(2)}) %collective-permute-start.17) | collective-permute-done | bytes 134176 | tf_op jit(solution)/shard_map/ppermute | solution.py:23
  (567 shorter events, 140.8 us)
Async XLA Ops:
  0.6 185.4 %copy-start = (bf16[1024,128]{1,0:T(8,128)(2,1)S(1)}, bf16[1024,128]{1,0:T(8,128)(2,1)}, u32[]{:S(2)}) copy-start(bf16[1024,128]{1,0:T(8,128)(2,1)} %param.15) | copy-start | bytes 786436
  2.4 31.3 %collective-permute-start.7 = (bf16[1,1,1,2,128,128]{5,4,3,2,1,0:T(8,128)(2,1)S(1)}, bf16[1,1,1,2,128,128]{5,4,3,2,1,0:T(8,128)(2,1)S(1)}, u32[]{:S(2)}, u32[]{:S(2)}) collective-permute-start(bf16[1,1,1,2,128,128]{5,4,3,2,1,0:T(8,128)(2,1)S(1)} %broadcast_select_fusion), channel_id=1, source_target_pairs={{256,0},{512,256},{768,512},{257,1},{513,257},{769,513},{258,2},{5... | collective-permute-start | bytes 196616 | tf_op jit(solution)/shard_map/ppermute | solution.py:15
  5.0 29.9 %collective-permute-start.6 = (bf16[1,1,1,2,128,128]{5,4,3,2,1,0:T(8,128)(2,1)S(1)}, bf16[1,1,1,2,128,128]{5,4,3,2,1,0:T(8,128)(2,1)S(1)}, u32[]{:S(2)}, u32[]{:S(2)}) collective-permute-start(bf16[1,1,1,2,128,128]{5,4,3,2,1,0:T(8,128)(2,1)S(1)} %broadcast_select_fusion), channel_id=1, source_target_pairs={{0,256},{256,512},{512,768},{1,257},{257,513},{513,769},{2,258},{2... | collective-permute-start | bytes 196616 | tf_op jit(solution)/shard_map/ppermute | solution.py:12
  34.9 30.6 %collective-permute-start.9 = (bf16[3,1,1,2,128,128]{5,4,3,2,1,0:T(8,128)(2,1)S(1)}, bf16[3,1,1,2,128,128]{5,4,3,2,1,0:T(8,128)(2,1)S(1)}, u32[]{:S(2)}, u32[]{:S(2)}) collective-permute-start(bf16[3,1,1,2,128,128]{5,4,3,2,1,0:T(8,128)(2,1)S(1)} %pad_maximum_fusion.5), channel_id=1, source_target_pairs={{16,0},{32,16},{48,32},{64,48},{80,64},{96,80},{112,96},{128,112},... | collective-permute-start | bytes 589832 | tf_op jit(solution)/shard_map/ppermute | solution.py:15
  36.2 29.3 %collective-permute-start.8 = (bf16[3,1,1,2,128,128]{5,4,3,2,1,0:T(8,128)(2,1)S(1)}, bf16[3,1,1,2,128,128]{5,4,3,2,1,0:T(8,128)(2,1)S(1)}, u32[]{:S(2)}, u32[]{:S(2)}) collective-permute-start(bf16[3,1,1,2,128,128]{5,4,3,2,1,0:T(8,128)(2,1)S(1)} %pad_maximum_fusion.5), channel_id=1, source_target_pairs={{0,16},{16,32},{32,48},{48,64},{64,80},{80,96},{96,112},{112,128},... | collective-permute-start | bytes 589832 | tf_op jit(solution)/shard_map/ppermute | solution.py:12
  40.2 25.2 %collective-permute-start = (f32[1,1,1,2,3,128]{5,3,4,2,1,0:T(2,128)}, f32[1,1,1,2,3,128]{5,3,4,2,1,0:T(2,128)S(1)}, u32[]{:S(2)}, u32[]{:S(2)}) collective-permute-start(f32[1,1,1,2,3,128]{5,3,4,2,1,0:T(2,128)} %param.11), channel_id=1, source_target_pairs={{0,256},{256,512},{512,768},{1,257},{257,513},{513,769},{2,258},{2... | collective-permute-start | bytes 9224 | tf_op jit(solution)/shard_map/ppermute | solution.py:12
  63.5 23.5 %collective-permute-start.1 = (f32[1,1,1,2,3,128]{5,3,4,2,1,0:T(2,128)}, f32[1,1,1,2,3,128]{5,3,4,2,1,0:T(2,128)S(1)}, u32[]{:S(2)}, u32[]{:S(2)}) collective-permute-start(f32[1,1,1,2,3,128]{5,3,4,2,1,0:T(2,128)} %param.11), channel_id=1, source_target_pairs={{256,0},{512,256},{768,512},{257,1},{513,257},{769,513},{258,2},{5... | collective-permute-start | bytes 9224 | tf_op jit(solution)/shard_map/ppermute | solution.py:15
  65.6 38.9 %collective-permute-start.11 = (bf16[3,3,1,2,128,128]{5,4,3,2,1,0:T(8,128)(2,1)S(1)}, bf16[3,3,1,2,128,128]{5,4,3,2,1,0:T(8,128)(2,1)S(1)}, u32[]{:S(2)}, u32[]{:S(2)}) collective-permute-start(bf16[3,3,1,2,128,128]{5,4,3,2,1,0:T(8,128)(2,1)S(1)} %pad_maximum_fusion.3), channel_id=1, source_target_pairs={{1,0},{2,1},{3,2},{4,3},{5,4},{6,5},{7,6},{8,7},{9,8},{10,9},{11,1... | collective-permute-start | bytes 1769480 | tf_op jit(solution)/shard_map/ppermute | solution.py:15
  70.1 34.3 %collective-permute-start.10 = (bf16[3,3,1,2,128,128]{5,4,3,2,1,0:T(8,128)(2,1)S(1)}, bf16[3,3,1,2,128,128]{5,4,3,2,1,0:T(8,128)(2,1)S(1)}, u32[]{:S(2)}, u32[]{:S(2)}) collective-permute-start(bf16[3,3,1,2,128,128]{5,4,3,2,1,0:T(8,128)(2,1)S(1)} %pad_maximum_fusion.3), channel_id=1, source_target_pairs={{0,1},{1,2},{2,3},{3,4},{4,5},{5,6},{6,7},{7,8},{8,9},{9,10},{10,1... | collective-permute-start | bytes 1769480 | tf_op jit(solution)/shard_map/ppermute | solution.py:12
  87.0 5.3 %collective-permute-start.3 = (f32[3,1,1,2,3,128]{5,3,4,2,1,0:T(2,128)S(1)}, f32[3,1,1,2,3,128]{5,3,4,2,1,0:T(2,128)S(1)}, u32[]{:S(2)}, u32[]{:S(2)}) collective-permute-start(f32[3,1,1,2,3,128]{5,3,4,2,1,0:T(2,128)S(1)} %constant_dynamic-update-slice_fusion), channel_id=1, source_target_pairs={{16,0},{32,16},{48,32},{64,48},{80,64},{96,80},{112,96},{128,112},... | collective-permute-start | bytes 27656 | tf_op jit(solution)/shard_map/ppermute | solution.py:15
  88.3 4.8 %collective-permute-start.2 = (f32[3,1,1,2,3,128]{5,3,4,2,1,0:T(2,128)S(1)}, f32[3,1,1,2,3,128]{5,3,4,2,1,0:T(2,128)S(1)}, u32[]{:S(2)}, u32[]{:S(2)}) collective-permute-start(f32[3,1,1,2,3,128]{5,3,4,2,1,0:T(2,128)S(1)} %constant_dynamic-update-slice_fusion), channel_id=1, source_target_pairs={{0,16},{16,32},{32,48},{48,64},{64,80},{80,96},{96,112},{112,128},... | collective-permute-start | bytes 27656 | tf_op jit(solution)/shard_map/ppermute | solution.py:12
  93.1 7.9 %collective-permute-start.5 = (f32[3,3,1,2,3,128]{5,3,4,2,1,0:T(2,128)S(1)}, f32[3,3,1,2,3,128]{5,3,4,2,1,0:T(2,128)S(1)}, u32[]{:S(2)}, u32[]{:S(2)}) collective-permute-start(f32[3,3,1,2,3,128]{5,3,4,2,1,0:T(2,128)S(1)} %pad_maximum_fusion.7), channel_id=1, source_target_pairs={{1,0},{2,1},{3,2},{4,3},{5,4},{6,5},{7,6},{8,7},{9,8},{10,9},{11,1... | collective-permute-start | bytes 82952 | tf_op jit(solution)/shard_map/ppermute | solution.py:15
  97.6 6.7 %collective-permute-start.4 = (f32[3,3,1,2,3,128]{5,3,4,2,1,0:T(2,128)S(1)}, f32[3,3,1,2,3,128]{5,3,4,2,1,0:T(2,128)S(1)}, u32[]{:S(2)}, u32[]{:S(2)}) collective-permute-start(f32[3,3,1,2,3,128]{5,3,4,2,1,0:T(2,128)S(1)} %pad_maximum_fusion.7), channel_id=1, source_target_pairs={{0,1},{1,2},{2,3},{3,4},{4,5},{5,6},{6,7},{7,8},{8,9},{9,10},{10,1... | collective-permute-start | bytes 82952 | tf_op jit(solution)/shard_map/ppermute | solution.py:12
  104.4 1.6 copy-start.3
  183.4 2.1 copy-start.1
  185.0 1.0 copy-start.4
  187.5 2.1 copy-start.2
  191.4 2.1 copy-start.5
  337.0 19.4 %collective-permute-start.12 = (f32[3,3,1,2,16768]{4,3,2,1,0:T(2,128)S(1)}, f32[3,3,1,2,16768]{4,3,2,1,0:T(2,128)S(1)}, u32[]{:S(2)}, u32[]{:S(2)}) collective-permute-start(f32[3,3,1,2,16768]{4,3,2,1,0:T(2,128)S(1)} %get-tuple-element.461), channel_id=1, source_target_pairs={{0,1},{1,2},{2,3},{3,4},{4,5},{5,6},{6,7},{7,8},{8,9},{9,10},{10,1... | collective-permute-start | bytes 3621896 | tf_op jit(solution)/shard_map/ppermute | solution.py:23
  338.9 18.9 %collective-permute-start.13 = (f32[3,3,1,2,16768]{4,3,2,1,0:T(2,128)S(1)}, f32[3,3,1,2,16768]{4,3,2,1,0:T(2,128)S(1)}, u32[]{:S(2)}, u32[]{:S(2)}) collective-permute-start(f32[3,3,1,2,16768]{4,3,2,1,0:T(2,128)S(1)} %get-tuple-element.462), channel_id=1, source_target_pairs={{1,0},{2,1},{3,2},{4,3},{5,4},{6,5},{7,6},{8,7},{9,8},{10,9},{11,1... | collective-permute-start | bytes 3621896 | tf_op jit(solution)/shard_map/ppermute | solution.py:23
  360.0 8.4 %collective-permute-start.14 = (f32[3,1,1,2,16768]{4,3,2,1,0:T(2,128)S(1)}, f32[3,1,1,2,16768]{4,3,2,1,0:T(2,128)S(1)}, u32[]{:S(2)}, u32[]{:S(2)}) collective-permute-start(f32[3,1,1,2,16768]{4,3,2,1,0:T(2,128)S(1)} %get-tuple-element.463), channel_id=1, source_target_pairs={{0,16},{16,32},{32,48},{48,64},{64,80},{80,96},{96,112},{112,128},... | collective-permute-start | bytes 1207304 | tf_op jit(solution)/shard_map/ppermute | solution.py:23
  363.7 8.6 %collective-permute-start.15 = (f32[3,1,1,2,16768]{4,3,2,1,0:T(2,128)S(1)}, f32[3,1,1,2,16768]{4,3,2,1,0:T(2,128)S(1)}, u32[]{:S(2)}, u32[]{:S(2)}) collective-permute-start(f32[3,1,1,2,16768]{4,3,2,1,0:T(2,128)S(1)} %get-tuple-element.464), channel_id=1, source_target_pairs={{16,0},{32,16},{48,32},{64,48},{80,64},{96,80},{112,96},{128,112},... | collective-permute-start | bytes 1207304 | tf_op jit(solution)/shard_map/ppermute | solution.py:23
  372.6 16.6 %collective-permute-start.16 = (f32[1,1,1,2,16768]{4,3,2,1,0:T(2,128)S(1)}, f32[1,1,1,2,16768]{4,3,2,1,0:T(2,128)S(1)}, u32[]{:S(2)}, u32[]{:S(2)}) collective-permute-start(f32[1,1,1,2,16768]{4,3,2,1,0:T(2,128)S(1)} %get-tuple-element.467), channel_id=1, source_target_pairs={{0,256},{256,512},{512,768},{1,257},{257,513},{513,769},{2,258},{2... | collective-permute-start | bytes 402440 | tf_op jit(solution)/shard_map/ppermute | solution.py:23
  387.2 33.6 %collective-permute-start.17 = (f32[1,1,1,2,16768]{4,3,2,1,0:T(2,128)S(1)}, f32[1,1,1,2,16768]{4,3,2,1,0:T(2,128)S(1)}, u32[]{:S(2)}, u32[]{:S(2)}) collective-permute-start(f32[1,1,1,2,16768]{4,3,2,1,0:T(2,128)S(1)} %get-tuple-element.468), channel_id=1, source_target_pairs={{256,0},{512,256},{768,512},{257,1},{513,257},{769,513},{258,2},{5... | collective-permute-start | bytes 402440 | tf_op jit(solution)/shard_map/ppermute | solution.py:23
where the time goes:
time: 430 us; the launch traced here: 422 us
  starting transfers between devices  109 us (25%)
  local copies, waits for them, and re-layouts  90 us (21%)
  waiting for transfers between devices  72.1 us (17%)
  other arithmetic  63.1 us (15%)
  loops' own time  46.2 us (11%)
  matrix products  40.9 us (10%)
    ppermute x6, starting transfers between devices, extended(): lax.ppermute(lax.slice_in_dim(block, block.shape[dim] - width, None, axis...  63.7 us
    ppermute x6, waiting for transfers between devices, from_behind(): return lax.ppermute(block, axis, route)  52.4 us
    dynamic_update_slice x16, local copies, waits for them, and re-layouts, backward_pair(): lax.dynamic_update_index_in_dim(ghost_sum, ghost_sum[source_index] + ghos...  41.5 us
    ppermute x6, starting transfers between devices, from_behind(): return lax.ppermute(block, axis, route)  28.9 us
    another operation x1, loops' own time, device_terms(): lax.fori_loop(0, pair_count, forward_pair, jnp.zeros((tile_count, atom_co...  23.8 us
    another operation x1, loops' own time, device_terms(): return lax.fori_loop(0, pair_count, backward_pair, start_pair)  22.4 us
    dynamic_slice x32, local copies, waits for them, and re-layouts, locate(): target = neighbour_rows[tile_index, slot_index]  19.9 us
    add x16, other arithmetic, backward_pair(): ghost_sum[source_index] + ghost_part  18.4 us
  transfers between devices with their start and end apart: 18, of which 10 were waited for; matrix products, arithmetic and copies ran while one was open for 1% of the time, Pallas kernels for 0%

commit v1 on v0

v1 whole, which is shorter than its diff:
```python
import functools

import jax
import jax.numpy as jnp
from jax import lax
from jax.experimental import pallas as pl
from jax.experimental.pallas import tpu as pltpu
from jax.sharding import PartitionSpec as P

A = 128
C = 128
R = 4
S = 8
T = 2
NEAR = 27 * T
ROWS = 136
SCALING = (S * A) ** -0.5
CHUNK = 32


def extended(block, sides, width):
    for axis, dim in sides:
        count = lax.axis_size(axis)
        forward = [(i, i + 1) for i in range(count - 1)]
        backward = [(target, source) for source, target in forward]
        low = lax.ppermute(
            lax.slice_in_dim(block, block.shape[dim] - width, None, axis=dim), axis, forward
        )
        high = lax.ppermute(lax.slice_in_dim(block, 0, width, axis=dim), axis, backward)
        block = jnp.concatenate([low, block, high], axis=dim)
    return block


def from_behind(block, axis, distance):
    devices = range(lax.axis_size(axis))
    route = [(i - distance, i) for i in devices if i - distance in devices]
    return lax.ppermute(block, axis, route)


def fold_plane(buffer, axis_dim, sender):
    lower_plane = lax.slice_in_dim(buffer, 0, 1, axis=axis_dim)
    middle_plane = lax.slice_in_dim(buffer, 1, 2, axis=axis_dim)
    upper_plane = lax.slice_in_dim(buffer, 2, 3, axis=axis_dim)
    result = middle_plane
    for toward in (1, -1):
        result = result + sender(upper_plane if toward == 1 else lower_plane, toward)
    return result


def pair_geometry(near, own, base, size):
    offset = [near[m : m + 1, :] - own[m, pl.ds(base, size), :] for m in range(3)]
    square = offset[0] * offset[0] + offset[1] * offset[1] + offset[2] * offset[2]
    return offset, square


def tile_terms(
    t, nbr, counts, rates, pos, near_pos, near_feat, mix, readout,
    own, basis, stack, sums, inv, grad, gbuf, own_acc, contrib, contrib_force, own_force,
):
    for m in range(3):
        own[m] = jnp.transpose(jnp.broadcast_to(pos[t, m : m + 1, :], (A, A)))
        own_acc[m] = jnp.zeros((A, A), jnp.float32)

    def build(s, carry):
        n = nbr[t * S + s]
        source = jnp.maximum(n, 0)
        near = near_pos[source]
        lanes = pl.ds(pl.multiple_of(s * A, A), A)
        tile = near_feat[source]
        stack[lanes, :] = jnp.where(n >= 0, tile, jnp.zeros_like(tile))
        for base in range(0, A, CHUNK):
            offset, square = pair_geometry(near, own, base, CHUNK)
            for r in range(R):
                g = jnp.exp(-rates[r] * square)
                for m in range(4):
                    value = g if m == 0 else g * offset[m - 1]
                    row = (r * 4 + m) * A + base
                    basis[row : row + CHUNK, lanes] = value.astype(jnp.bfloat16)
        return carry

    lax.fori_loop(0, S, build, 0)

    def forward(k, carry):
        rows = pl.ds(pl.multiple_of(k * 4 * A, 4 * A), 4 * A)
        sums[rows, :] = jnp.dot(basis[rows, :], stack[...], preferred_element_type=jnp.float32) * SCALING
        return carry

    lax.fori_loop(0, R, forward, 0)

    for r in range(R):
        base = r * 4 * A
        inv[:, r * C : (r + 1) * C] = sums[base : base + A, :].astype(jnp.bfloat16)
        total = jnp.zeros((A, C), jnp.float32)
        for m in range(1, 4):
            part = sums[base + m * A : base + (m + 1) * A, :]
            total = total + part * part
        inv[:, (R + r) * C : (R + r + 1) * C] = total.astype(jnp.bfloat16)
    preact = jnp.dot(inv[...], mix[...], preferred_element_type=jnp.float32)
    sigmoid = 1.0 / (1.0 + jnp.exp(-preact))
    valid = lax.broadcasted_iota(jnp.int32, (A, C), 0) < counts[t]
    grad_pre = readout[...] * sigmoid * (1.0 + preact * (1.0 - sigmoid))
    grad_pre = jnp.where(valid, grad_pre, 0.0).astype(jnp.bfloat16)
    for r in range(R):
        base = r * 4 * A
        for half in range(2):
            k = half * R + r
            gi = lax.dot_general(
                grad_pre, mix[k * C : (k + 1) * C, :], (((1,), (1,)), ((), ())),
                preferred_element_type=jnp.float32,
            )
            if half == 0:
                grad[base : base + A, :] = (gi * SCALING).astype(jnp.bfloat16)
            else:
                for m in range(1, 4):
                    rows = slice(base + m * A, base + (m + 1) * A)
                    grad[rows, :] = (2.0 * sums[rows, :] * gi * SCALING).astype(jnp.bfloat16)

    def backward(p, carry):
        wide = pl.ds(pl.multiple_of(p * 2 * A, 2 * A), 2 * A)
        near_grad = lax.dot_general(
            basis[:, wide], grad[...], (((0,), (0,)), ((), ())), preferred_element_type=jnp.float32
        )
        pair = t * S + p * 2
        contrib[pair] = near_grad[:A]
        contrib[pair + 1] = near_grad[A:]
        gbuf[...] = lax.dot_general(
            grad[...], stack[wide, :], (((1,), (1,)), ((), ())), preferred_element_type=jnp.float32
        )
        for u in range(2):
            near = near_pos[jnp.maximum(nbr[pair + u], 0)]
            cols = slice(u * A, (u + 1) * A)
            column = [jnp.zeros((8, A), jnp.float32) for _ in range(3)]
            for base in range(0, A, CHUNK):
                offset, square = pair_geometry(near, own, base, CHUNK)
                force = [None] * 3
                pull = None
                for r in range(R):
                    g = jnp.exp(-rates[r] * square)
                    gb = [gbuf[(r * 4 + m) * A + base : (r * 4 + m) * A + base + CHUNK, cols] for m in range(4)]
                    inner = gb[0] + gb[1] * offset[0] + gb[2] * offset[1] + gb[3] * offset[2]
                    term = (2.0 * rates[r]) * g * inner
                    pull = term if pull is None else pull + term
                    for m in range(3):
                        part = g * gb[m + 1]
                        force[m] = part if force[m] is None else force[m] + part
                for m in range(3):
                    force[m] = force[m] - offset[m] * pull
                    own_acc[m, base : base + CHUNK, :] += force[m]
                    for k in range(0, CHUNK, 8):
                        column[m] = column[m] + force[m][k : k + 8]
            for m in range(3):
                contrib_force[pair + u, m : m + 1, :] = -jnp.sum(column[m], axis=0, keepdims=True)
        return carry

    lax.fori_loop(0, S // 2, backward, 0)
    for m in range(3):
        own_force[t, m : m + 1, :] = jnp.sum(jnp.transpose(own_acc[m]), axis=0, keepdims=True)


def compute_kernel(
    nbr, inverse, counts, rates, pos, near_pos, near_feat, mix, readout,
    own_force, ghost,
    own, basis, stack, sums, inv, grad, gbuf, own_acc, contrib, contrib_force,
):
    def one_tile(t, carry):
        tile_terms(
            t, nbr, counts, rates, pos, near_pos, near_feat, mix, readout,
            own, basis, stack, sums, inv, grad, gbuf, own_acc, contrib, contrib_force, own_force,
        )
        return carry

    lax.fori_loop(0, T, one_tile, 0)

    def gather(n, carry):
        block = jnp.zeros((A, C), jnp.float32)
        force = jnp.zeros((8, A), jnp.float32)
        for t in range(T):
            s = inverse[t * NEAR + n]
            pair = t * S + jnp.maximum(s, 0)
            block = block + jnp.where(s >= 0, contrib[pair], 0.0)
            force = force + jnp.where(s >= 0, contrib_force[pair], 0.0)
        ghost[n, 0:A, :] = block
        ghost[n, A:ROWS, :] = force
        return carry

    lax.fori_loop(0, NEAR, gather, 0)


def compute(nbr, counts, rates, pos, near_pos, near_feat, mix, readout):
    flat = nbr.reshape(T * S)
    where = jnp.where(
        nbr[:, :, None] == lax.broadcasted_iota(jnp.int32, (T, S, NEAR), 2),
        lax.broadcasted_iota(jnp.int32, (T, S, NEAR), 1),
        -1,
    )
    inverse = jnp.max(where, axis=1).reshape(T * NEAR)
    smem = pl.BlockSpec(memory_space=pltpu.SMEM)
    vmem = pl.BlockSpec(memory_space=pltpu.VMEM)
    return pl.pallas_call(
        compute_kernel,
        out_shape=(
            jax.ShapeDtypeStruct((T, 3, A), jnp.float32),
            jax.ShapeDtypeStruct((NEAR, ROWS, C), jnp.float32),
        ),
        in_specs=[smem] * 4 + [vmem] * 5,
        out_specs=(vmem, vmem),
        scratch_shapes=[
            pltpu.VMEM((3, A, A), jnp.float32),
            pltpu.VMEM((4 * R * A, S * A), jnp.bfloat16),
            pltpu.VMEM((S * A, C), jnp.bfloat16),
            pltpu.VMEM((4 * R * A, C), jnp.float32),
            pltpu.VMEM((A, 2 * R * C), jnp.bfloat16),
            pltpu.VMEM((4 * R * A, C), jnp.bfloat16),
            pltpu.VMEM((4 * R * A, 2 * A), jnp.float32),
            pltpu.VMEM((3, A, A), jnp.float32),
            pltpu.VMEM((T * S, A, C), jnp.float32),
            pltpu.VMEM((T * S, 8, A), jnp.float32),
        ],
        compiler_params=pltpu.CompilerParams(vmem_limit_bytes=48 * 1024 * 1024),
    )(flat, inverse, counts, rates, pos, near_pos, near_feat, mix, readout)


def body(positions, features, counts, neighbours, mix_weight, readout, radial_rates):
    own_counts = counts.reshape(T)
    is_valid = lax.broadcasted_iota(jnp.int32, (T, A), 1) < own_counts[:, None]
    masked = jnp.where(is_valid.reshape(1, 1, 1, T, A, 1), features, jnp.zeros((), jnp.bfloat16))
    near_points = extended(positions, (("gx", 0), ("gy", 1), ("gz", 2)), 1)
    near_features = extended(masked, (("gx", 0), ("gy", 1), ("gz", 2)), 1)
    own_force, ghost = compute(
        neighbours.reshape(T, S),
        own_counts,
        radial_rates,
        positions.reshape(T, 3, A),
        near_points.reshape(NEAR, 3, A),
        near_features.reshape(NEAR, A, C),
        mix_weight,
        readout.reshape(1, C),
    )
    buffer = ghost.reshape(3, 3, 3, T, ROWS, C)
    buffer = fold_plane(buffer, 2, lambda values, toward: from_behind(values, "gz", toward))
    buffer = fold_plane(buffer, 1, lambda values, toward: from_behind(values, "gy", toward))
    buffer = fold_plane(buffer, 0, lambda values, toward: from_behind(values, "gx", toward))
    center = buffer.reshape(T, ROWS, C)
    forces = own_force + center[:, A : A + 3, :]
    feature_grads = jnp.where(is_valid[:, :, None], center[:, :A, :], 0.0)
    return (
        forces.reshape(1, 1, 1, T, 3, A),
        feature_grads.reshape(1, 1, 1, T, A, C),
    )


def solution(mesh):
    cell = ("gx", "gy", "gz")
    in_specs = (
        P(*cell, None, None, None),
        P(*cell, None, None, None),
        P(*cell, None),
        P(*cell, None, None),
        P(),
        P(),
        P(),
    )
    out_specs = (P(*cell, None, None, None), P(*cell, None, None, None))
    return jax.shard_map(body, mesh=mesh, in_specs=in_specs, out_specs=out_specs, check_vma=False)
```

time: 430 us -> 210 us (0.49); the launches traced: 422 us -> 207 us
  local copies, waits for them, and re-layouts: 90 us -> 2.37 us
  other arithmetic: 63.1 us -> 3.31 us
  loops' own time: 46.2 us -> 0 us
  matrix products: 40.9 us -> 0 us
  Pallas kernels: 0 us -> 17.4 us
    another operation x2 -> x0, loops' own time: 46.2 us -> none  [the longest x1 23.8 us: device_terms(): lax.fori_loop(0, pair_count, forward_pair, jnp.zeros((tile_count, atom_co...]
    dynamic_update_slice x48 -> x0, local copies, waits for them, and re-layouts: 42.2 us -> none  [the longest x16 41.5 us: backward_pair(): lax.dynamic_update_index_in_dim(ghost_sum, ghost_sum[source_index] + ghos...]
    dot_general x49 -> x0, matrix products: 40.9 us -> none  [the longest x16 17.2 us: backward_pair(): lax.dot_general(seed_rows, near_tile, (((1,), (1,)), ((), ())), preferred...]
    dynamic_slice x80 -> x0, local copies, waits for them, and re-layouts: 22 us -> none  [the longest x32 19.9 us: locate(): target = neighbour_rows[tile_index, slot_index]]
    add x16 -> x0, other arithmetic: 18.4 us -> none  [backward_pair(): ghost_sum[source_index] + ghost_part]
    pallas_call x0 -> x1, Pallas kernels: none -> 17.4 us  [compute(): pl.pallas_call(compute_kernel, out_shape=(jax.ShapeDtypeStruct((T, 3, A),...]
    reduce_sum x65 -> x0, other arithmetic: 12.1 us -> none  [the longest x16 5.6 us: backward_pair(): jnp.sum(pair_force, axis=0).reshape(-1)]
    concatenate x33 -> x0, other arithmetic: 9.8 us -> none  [the longest x32 9.52 us: build_basis(): jnp.concatenate([radial[:, :, None, :], radial[:, :, None, :] * offset[:,...]
  transfers between devices with their start and end apart: 18 -> 18, of which waited for: 10 -> 11; matrix products, arithmetic and copies ran while one was open for 1% -> 1% of each run, Pallas kernels for 0% -> 0%
where the time goes in v1:
time: 210 us; the launch traced here: 207 us
  starting transfers between devices  109 us (52%)
  waiting for transfers between devices  74.4 us (35%)
  Pallas kernels  17.4 us (8%)
  other arithmetic  3.31 us (2%)
  local copies, waits for them, and re-layouts  2.37 us (1%)
    ppermute x6, starting transfers between devices, extended(): lax.ppermute(lax.slice_in_dim(block, block.shape[dim] - width, None, axis...  63.7 us
    ppermute x6, waiting for transfers between devices, from_behind(): return lax.ppermute(block, axis, route)  53.5 us
    ppermute x6, starting transfers between devices, from_behind(): return lax.ppermute(block, axis, route)  28.9 us
    pallas_call x1, Pallas kernels, compute(): pl.pallas_call(compute_kernel, out_shape=(jax.ShapeDtypeStruct((T, 3, A),...  17.4 us
    ppermute x6, starting transfers between devices, extended(): lax.ppermute(lax.slice_in_dim(block, 0, width, axis=dim), axis, backward)  16.2 us
    ppermute x6, waiting for transfers between devices, extended(): lax.ppermute(lax.slice_in_dim(block, 0, width, axis=dim), axis, backward)  14.3 us
    ppermute x6, waiting for transfers between devices, extended(): lax.ppermute(lax.slice_in_dim(block, block.shape[dim] - width, None, axis...  6.5 us
  transfers between devices with their start and end apart: 18, of which 11 were waited for; matrix products, arithmetic and copies ran while one was open for 1% of the time, Pallas kernels for 0%

profile of v1, /device:TPU:25, one launch (start us, length us, event | category | flops | bytes accessed | tf_op | source)
XLA Modules:
  0.0 207.3 jit_solution(3404624037064389435)
XLA Ops:
  0.6 0.0 copy-start.4
  0.7 0.7 iota_compare_fusion.1
  1.4 0.9 broadcast_select_fusion
  2.3 2.6 %collective-permute-start.7 = (bf16[1,1,1,2,128,128]{5,4,3,2,1,0:T(8,128)(2,1)S(1)}, bf16[1,1,1,2,128,128]{5,4,3,2,1,0:T(8,128)(2,1)S(1)}, u32[]{:S(2)}, u32[]{:S(2)}) collective-permute-start(bf16[1,1,1,2,128,128]{5,4,3,2,1,0:T(8,128)(2,1)S(1)} %broadcast_select_fusion), channel_id=1, source_target_pairs={{256,0},{512,256},{768,512},{257,1},{513,257},{769,513},{258,2},{5... | collective-permute-start | bytes 196616 | tf_op jit(solution)/shard_map/ppermute | solution.py:29
  4.9 28.6 %collective-permute-start.6 = (bf16[1,1,1,2,128,128]{5,4,3,2,1,0:T(8,128)(2,1)S(1)}, bf16[1,1,1,2,128,128]{5,4,3,2,1,0:T(8,128)(2,1)S(1)}, u32[]{:S(2)}, u32[]{:S(2)}) collective-permute-start(bf16[1,1,1,2,128,128]{5,4,3,2,1,0:T(8,128)(2,1)S(1)} %broadcast_select_fusion), channel_id=1, source_target_pairs={{0,256},{256,512},{512,768},{1,257},{257,513},{513,769},{2,258},{2... | collective-permute-start | bytes 196616 | tf_op jit(solution)/shard_map/ppermute | solution.py:26
  33.5 0.1 collective-permute-done.7
  33.6 1.2 collective-permute-done.6
  34.9 1.3 collective-permute-start.9
  36.2 4.0 %collective-permute-start.8 = (bf16[3,1,1,2,128,128]{5,4,3,2,1,0:T(8,128)(2,1)S(1)}, bf16[3,1,1,2,128,128]{5,4,3,2,1,0:T(8,128)(2,1)S(1)}, u32[]{:S(2)}, u32[]{:S(2)}) collective-permute-start(bf16[3,1,1,2,128,128]{5,4,3,2,1,0:T(8,128)(2,1)S(1)} %pad_maximum_fusion.2), channel_id=1, source_target_pairs={{0,16},{16,32},{32,48},{48,64},{64,80},{80,96},{96,112},{112,128},... | collective-permute-start | bytes 589832 | tf_op jit(solution)/shard_map/ppermute | solution.py:26
  40.2 23.3 %collective-permute-start = (f32[1,1,1,2,3,128]{5,3,4,2,1,0:T(2,128)}, f32[1,1,1,2,3,128]{5,3,4,2,1,0:T(2,128)S(1)}, u32[]{:S(2)}, u32[]{:S(2)}) collective-permute-start(f32[1,1,1,2,3,128]{5,3,4,2,1,0:T(2,128)} %param.7), channel_id=1, source_target_pairs={{0,256},{256,512},{512,768},{1,257},{257,513},{513,769},{2,258},{2... | collective-permute-start | bytes 9224 | tf_op jit(solution)/shard_map/ppermute | solution.py:26
  63.5 1.9 collective-permute-start.1
  65.4 0.1 pad_maximum_fusion.1
  65.5 4.6 %collective-permute-start.11 = (bf16[3,3,1,2,128,128]{5,4,3,2,1,0:T(8,128)(2,1)S(1)}, bf16[3,3,1,2,128,128]{5,4,3,2,1,0:T(8,128)(2,1)S(1)}, u32[]{:S(2)}, u32[]{:S(2)}) collective-permute-start(bf16[3,3,1,2,128,128]{5,4,3,2,1,0:T(8,128)(2,1)S(1)} %pad_maximum_fusion.1), channel_id=1, source_target_pairs={{1,0},{2,1},{3,2},{4,3},{5,4},{6,5},{7,6},{8,7},{9,8},{10,9},{11,1... | collective-permute-start | bytes 1769480 | tf_op jit(solution)/shard_map/ppermute | solution.py:29
  70.1 1.9 collective-permute-start.10
  72.0 0.7 constant_dynamic-update-slice_fusion.1
  72.7 14.2 %collective-permute-done.1 = f32[1,1,1,2,3,128]{5,3,4,2,1,0:T(2,128)S(1)} collective-permute-done((f32[1,1,1,2,3,128]{5,3,4,2,1,0:T(2,128)}, f32[1,1,1,2,3,128]{5,3,4,2,1,0:T(2,128)S(1)}, u32[]{:S(2)}, u32[]{:S(2)}) %collective-permute-start.1) | collective-permute-done | bytes 3104 | tf_op jit(solution)/shard_map/ppermute | solution.py:29
  87.0 1.3 collective-permute-start.3
  88.2 4.0 %collective-permute-start.2 = (f32[3,1,1,2,3,128]{5,3,4,2,1,0:T(2,128)S(1)}, f32[3,1,1,2,3,128]{5,3,4,2,1,0:T(2,128)S(1)}, u32[]{:S(2)}, u32[]{:S(2)}) collective-permute-start(f32[3,1,1,2,3,128]{5,3,4,2,1,0:T(2,128)S(1)} %constant_dynamic-update-slice_fusion), channel_id=1, source_target_pairs={{0,16},{16,32},{32,48},{48,64},{64,80},{80,96},{96,112},{112,128},... | collective-permute-start | bytes 27656 | tf_op jit(solution)/shard_map/ppermute | solution.py:26
  92.2 0.8 collective-permute-done.2
  93.0 4.6 %collective-permute-start.5 = (f32[3,3,1,2,3,128]{5,3,4,2,1,0:T(2,128)S(1)}, f32[3,3,1,2,3,128]{5,3,4,2,1,0:T(2,128)S(1)}, u32[]{:S(2)}, u32[]{:S(2)}) collective-permute-start(f32[3,3,1,2,3,128]{5,3,4,2,1,0:T(2,128)S(1)} %pad_maximum_fusion.4), channel_id=1, source_target_pairs={{1,0},{2,1},{3,2},{4,3},{5,4},{6,5},{7,6},{8,7},{9,8},{10,9},{11,1... | collective-permute-start | bytes 82952 | tf_op jit(solution)/shard_map/ppermute | solution.py:29
  97.6 1.9 collective-permute-start.4
  99.5 0.1 select_reduce_fusion
  99.6 0.1 reshape_reshape.3.nbr
  99.7 0.1 reshape.79.inverse
  99.8 4.5 %collective-permute-done.4 = f32[3,3,1,2,3,128]{5,3,4,2,1,0:T(2,128)S(1)} collective-permute-done((f32[3,3,1,2,3,128]{5,3,4,2,1,0:T(2,128)S(1)}, f32[3,3,1,2,3,128]{5,3,4,2,1,0:T(2,128)S(1)}, u32[]{:S(2)}, u32[]{:S(2)}) %collective-permute-start.4) | collective-permute-done | bytes 27680 | tf_op jit(solution)/shard_map/ppermute | solution.py:26
  104.4 0.0 copy-start
  104.4 0.0 copy-start.3
  104.5 0.3 pad_maximum_fusion
  104.7 0.6 copy-done
  105.4 17.4 %shard_map.86 = (f32[2,3,128]{2,1,0:T(4,128)S(1)}, f32[54,136,128]{2,1,0:T(8,128)S(1)}) custom-call(s32[16]{0:T(128)S(1)} %reshape_reshape.3.nbr, s32[108]{0:T(128)S(1)} %reshape.79.inverse, s32[2]{0:T(128)S(1)} %bitcast.21, f32[4]{0:T(128)S(1)} %copy-done.2, f32[2,3,128]{2,1,0:T(4,128)S(1)} %bitcast.19, f32[54,3,128]{2,1,0:T(4,128)S(1)} %bitcast.18, ...), custom_call_target="tpu_custom_call" | custom-call | tf_op jit(solution)/shard_map/pallas_call | solution.py:199
  122.7 0.2 fusion.6
  122.9 1.9 collective-permute-start.12
  124.8 5.5 %collective-permute-start.13 = (f32[3,3,1,2,136,128]{5,4,3,2,1,0:T(8,128)S(1)}, f32[3,3,1,2,136,128]{5,4,3,2,1,0:T(8,128)S(1)}, u32[]{:S(2)}, u32[]{:S(2)}) collective-permute-start(f32[3,3,1,2,136,128]{5,4,3,2,1,0:T(8,128)S(1)} %get-tuple-element.11), channel_id=1, source_target_pairs={{1,0},{2,1},{3,2},{4,3},{5,4},{6,5},{7,6},{8,7},{9,8},{10,9},{11,1... | collective-permute-start | bytes 3760136 | tf_op jit(solution)/shard_map/ppermute | solution.py:37
  130.3 12.4 %collective-permute-done.12 = f32[3,3,1,2,136,128]{5,4,3,2,1,0:T(8,128)S(1)} collective-permute-done((f32[3,3,1,2,136,128]{5,4,3,2,1,0:T(8,128)S(1)}, f32[3,3,1,2,136,128]{5,4,3,2,1,0:T(8,128)S(1)}, u32[]{:S(2)}, u32[]{:S(2)}) %collective-permute-start.12) | collective-permute-done | bytes 1253408 | tf_op jit(solution)/shard_map/ppermute | solution.py:37
  142.8 1.5 collective-permute-done.13
  144.2 0.3 fusion
  144.5 0.1 fusion.7
  144.6 3.7 %collective-permute-start.14 = (f32[3,1,1,2,136,128]{5,4,3,2,1,0:T(8,128)S(1)}, f32[3,1,1,2,136,128]{5,4,3,2,1,0:T(8,128)S(1)}, u32[]{:S(2)}, u32[]{:S(2)}) collective-permute-start(f32[3,1,1,2,136,128]{5,4,3,2,1,0:T(8,128)S(1)} %get-tuple-element.12), channel_id=1, source_target_pairs={{0,16},{16,32},{32,48},{48,64},{64,80},{80,96},{96,112},{112,128},... | collective-permute-start | bytes 1253384 | tf_op jit(solution)/shard_map/ppermute | solution.py:37
  148.2 1.3 collective-permute-start.15
  149.5 3.6 %collective-permute-done.14 = f32[3,1,1,2,136,128]{5,4,3,2,1,0:T(8,128)S(1)} collective-permute-done((f32[3,1,1,2,136,128]{5,4,3,2,1,0:T(8,128)S(1)}, f32[3,1,1,2,136,128]{5,4,3,2,1,0:T(8,128)S(1)}, u32[]{:S(2)}, u32[]{:S(2)}) %collective-permute-start.14) | collective-permute-done | bytes 417824 | tf_op jit(solution)/shard_map/ppermute | solution.py:37
  153.2 3.8 %collective-permute-done.15 = f32[3,1,1,2,136,128]{5,4,3,2,1,0:T(8,128)S(1)} collective-permute-done((f32[3,1,1,2,136,128]{5,4,3,2,1,0:T(8,128)S(1)}, f32[3,1,1,2,136,128]{5,4,3,2,1,0:T(8,128)S(1)}, u32[]{:S(2)}, u32[]{:S(2)}) %collective-permute-start.15) | collective-permute-done | bytes 417824 | tf_op jit(solution)/shard_map/ppermute | solution.py:37
  157.0 0.1 fusion.1
  157.1 14.7 %collective-permute-start.16 = (f32[1,1,1,2,136,128]{5,4,3,2,1,0:T(8,128)S(1)}, f32[1,1,1,2,136,128]{5,4,3,2,1,0:T(8,128)S(1)}, u32[]{:S(2)}, u32[]{:S(2)}) collective-permute-start(f32[1,1,1,2,136,128]{5,4,3,2,1,0:T(8,128)S(1)} %get-tuple-element.14), channel_id=1, source_target_pairs={{0,256},{256,512},{512,768},{1,257},{257,513},{513,769},{2,258},{2... | collective-permute-start | bytes 417800 | tf_op jit(solution)/shard_map/ppermute | solution.py:37
  171.8 1.9 collective-permute-start.17
  173.7 0.1 collective-permute-done.16
  173.8 32.1 %collective-permute-done.17 = f32[1,1,1,2,136,128]{5,4,3,2,1,0:T(8,128)S(1)} collective-permute-done((f32[1,1,1,2,136,128]{5,4,3,2,1,0:T(8,128)S(1)}, f32[1,1,1,2,136,128]{5,4,3,2,1,0:T(8,128)S(1)}, u32[]{:S(2)}, u32[]{:S(2)}) %collective-permute-start.17) | collective-permute-done | bytes 139296 | tf_op jit(solution)/shard_map/ppermute | solution.py:37
  205.9 0.8 fusion.4
  206.7 0.6 copy.14
  (25 shorter events, 0.2 us)
Async XLA Ops:
  0.6 99.1 %copy-start.4 = (f32[1,1,1,2,3,128]{5,3,4,2,1,0:T(2,128)S(1)}, f32[1,1,1,2,3,128]{5,3,4,2,1,0:T(2,128)}, u32[]{:S(2)}) copy-start(f32[1,1,1,2,3,128]{5,3,4,2,1,0:T(2,128)} %param.7) | copy-start | bytes 9220
  0.6 98.9 %copy-start.5 = (s32[1,1,1,2,8]{4,3,2,1,0:T(2,128)S(1)}, s32[1,1,1,2,8]{4,3,2,1,0:T(2,128)}, u32[]{:S(2)}) copy-start(s32[1,1,1,2,8]{4,3,2,1,0:T(2,128)} %param.10) | copy-start | bytes 196
  2.3 31.3 %collective-permute-start.7 = (bf16[1,1,1,2,128,128]{5,4,3,2,1,0:T(8,128)(2,1)S(1)}, bf16[1,1,1,2,128,128]{5,4,3,2,1,0:T(8,128)(2,1)S(1)}, u32[]{:S(2)}, u32[]{:S(2)}) collective-permute-start(bf16[1,1,1,2,128,128]{5,4,3,2,1,0:T(8,128)(2,1)S(1)} %broadcast_select_fusion), channel_id=1, source_target_pairs={{256,0},{512,256},{768,512},{257,1},{513,257},{769,513},{258,2},{5... | collective-permute-start | bytes 196616 | tf_op jit(solution)/shard_map/ppermute | solution.py:29
  4.9 29.9 %collective-permute-start.6 = (bf16[1,1,1,2,128,128]{5,4,3,2,1,0:T(8,128)(2,1)S(1)}, bf16[1,1,1,2,128,128]{5,4,3,2,1,0:T(8,128)(2,1)S(1)}, u32[]{:S(2)}, u32[]{:S(2)}) collective-permute-start(bf16[1,1,1,2,128,128]{5,4,3,2,1,0:T(8,128)(2,1)S(1)} %broadcast_select_fusion), channel_id=1, source_target_pairs={{0,256},{256,512},{512,768},{1,257},{257,513},{513,769},{2,258},{2... | collective-permute-start | bytes 196616 | tf_op jit(solution)/shard_map/ppermute | solution.py:26
  34.9 30.6 %collective-permute-start.9 = (bf16[3,1,1,2,128,128]{5,4,3,2,1,0:T(8,128)(2,1)S(1)}, bf16[3,1,1,2,128,128]{5,4,3,2,1,0:T(8,128)(2,1)S(1)}, u32[]{:S(2)}, u32[]{:S(2)}) collective-permute-start(bf16[3,1,1,2,128,128]{5,4,3,2,1,0:T(8,128)(2,1)S(1)} %pad_maximum_fusion.2), channel_id=1, source_target_pairs={{16,0},{32,16},{48,32},{64,48},{80,64},{96,80},{112,96},{128,112},... | collective-permute-start | bytes 589832 | tf_op jit(solution)/shard_map/ppermute | solution.py:29
  36.2 29.3 %collective-permute-start.8 = (bf16[3,1,1,2,128,128]{5,4,3,2,1,0:T(8,128)(2,1)S(1)}, bf16[3,1,1,2,128,128]{5,4,3,2,1,0:T(8,128)(2,1)S(1)}, u32[]{:S(2)}, u32[]{:S(2)}) collective-permute-start(bf16[3,1,1,2,128,128]{5,4,3,2,1,0:T(8,128)(2,1)S(1)} %pad_maximum_fusion.2), channel_id=1, source_target_pairs={{0,16},{16,32},{32,48},{48,64},{64,80},{80,96},{96,112},{112,128},... | collective-permute-start | bytes 589832 | tf_op jit(solution)/shard_map/ppermute | solution.py:26
  40.2 31.9 %collective-permute-start = (f32[1,1,1,2,3,128]{5,3,4,2,1,0:T(2,128)}, f32[1,1,1,2,3,128]{5,3,4,2,1,0:T(2,128)S(1)}, u32[]{:S(2)}, u32[]{:S(2)}) collective-permute-start(f32[1,1,1,2,3,128]{5,3,4,2,1,0:T(2,128)} %param.7), channel_id=1, source_target_pairs={{0,256},{256,512},{512,768},{1,257},{257,513},{513,769},{2,258},{2... | collective-permute-start | bytes 9224 | tf_op jit(solution)/shard_map/ppermute | solution.py:26
  63.5 23.5 %collective-permute-start.1 = (f32[1,1,1,2,3,128]{5,3,4,2,1,0:T(2,128)}, f32[1,1,1,2,3,128]{5,3,4,2,1,0:T(2,128)S(1)}, u32[]{:S(2)}, u32[]{:S(2)}) collective-permute-start(f32[1,1,1,2,3,128]{5,3,4,2,1,0:T(2,128)} %param.7), channel_id=1, source_target_pairs={{256,0},{512,256},{768,512},{257,1},{513,257},{769,513},{258,2},{5... | collective-permute-start | bytes 9224 | tf_op jit(solution)/shard_map/ppermute | solution.py:29
  65.5 38.9 %collective-permute-start.11 = (bf16[3,3,1,2,128,128]{5,4,3,2,1,0:T(8,128)(2,1)S(1)}, bf16[3,3,1,2,128,128]{5,4,3,2,1,0:T(8,128)(2,1)S(1)}, u32[]{:S(2)}, u32[]{:S(2)}) collective-permute-start(bf16[3,3,1,2,128,128]{5,4,3,2,1,0:T(8,128)(2,1)S(1)} %pad_maximum_fusion.1), channel_id=1, source_target_pairs={{1,0},{2,1},{3,2},{4,3},{5,4},{6,5},{7,6},{8,7},{9,8},{10,9},{11,1... | collective-permute-start | bytes 1769480 | tf_op jit(solution)/shard_map/ppermute | solution.py:29
  70.1 34.4 %collective-permute-start.10 = (bf16[3,3,1,2,128,128]{5,4,3,2,1,0:T(8,128)(2,1)S(1)}, bf16[3,3,1,2,128,128]{5,4,3,2,1,0:T(8,128)(2,1)S(1)}, u32[]{:S(2)}, u32[]{:S(2)}) collective-permute-start(bf16[3,3,1,2,128,128]{5,4,3,2,1,0:T(8,128)(2,1)S(1)} %pad_maximum_fusion.1), channel_id=1, source_target_pairs={{0,1},{1,2},{2,3},{3,4},{4,5},{5,6},{6,7},{7,8},{8,9},{9,10},{10,1... | collective-permute-start | bytes 1769480 | tf_op jit(solution)/shard_map/ppermute | solution.py:26
  87.0 5.3 %collective-permute-start.3 = (f32[3,1,1,2,3,128]{5,3,4,2,1,0:T(2,128)S(1)}, f32[3,1,1,2,3,128]{5,3,4,2,1,0:T(2,128)S(1)}, u32[]{:S(2)}, u32[]{:S(2)}) collective-permute-start(f32[3,1,1,2,3,128]{5,3,4,2,1,0:T(2,128)S(1)} %constant_dynamic-update-slice_fusion), channel_id=1, source_target_pairs={{16,0},{32,16},{48,32},{64,48},{80,64},{96,80},{112,96},{128,112},... | collective-permute-start | bytes 27656 | tf_op jit(solution)/shard_map/ppermute | solution.py:29
  88.2 4.8 %collective-permute-start.2 = (f32[3,1,1,2,3,128]{5,3,4,2,1,0:T(2,128)S(1)}, f32[3,1,1,2,3,128]{5,3,4,2,1,0:T(2,128)S(1)}, u32[]{:S(2)}, u32[]{:S(2)}) collective-permute-start(f32[3,1,1,2,3,128]{5,3,4,2,1,0:T(2,128)S(1)} %constant_dynamic-update-slice_fusion), channel_id=1, source_target_pairs={{0,16},{16,32},{32,48},{48,64},{64,80},{80,96},{96,112},{112,128},... | collective-permute-start | bytes 27656 | tf_op jit(solution)/shard_map/ppermute | solution.py:26
  93.0 6.8 %collective-permute-start.5 = (f32[3,3,1,2,3,128]{5,3,4,2,1,0:T(2,128)S(1)}, f32[3,3,1,2,3,128]{5,3,4,2,1,0:T(2,128)S(1)}, u32[]{:S(2)}, u32[]{:S(2)}) collective-permute-start(f32[3,3,1,2,3,128]{5,3,4,2,1,0:T(2,128)S(1)} %pad_maximum_fusion.4), channel_id=1, source_target_pairs={{1,0},{2,1},{3,2},{4,3},{5,4},{6,5},{7,6},{8,7},{9,8},{10,9},{11,1... | collective-permute-start | bytes 82952 | tf_op jit(solution)/shard_map/ppermute | solution.py:29
  97.6 6.7 %collective-permute-start.4 = (f32[3,3,1,2,3,128]{5,3,4,2,1,0:T(2,128)S(1)}, f32[3,3,1,2,3,128]{5,3,4,2,1,0:T(2,128)S(1)}, u32[]{:S(2)}, u32[]{:S(2)}) collective-permute-start(f32[3,3,1,2,3,128]{5,3,4,2,1,0:T(2,128)S(1)} %pad_maximum_fusion.4), channel_id=1, source_target_pairs={{0,1},{1,2},{2,3},{3,4},{4,5},{5,6},{6,7},{7,8},{8,9},{9,10},{10,1... | collective-permute-start | bytes 82952 | tf_op jit(solution)/shard_map/ppermute | solution.py:26
  104.4 1.0 copy-start
  104.4 0.9 copy-start.1
  104.4 0.9 copy-start.2
  104.4 0.9 copy-start.3
  122.9 19.8 %collective-permute-start.12 = (f32[3,3,1,2,136,128]{5,4,3,2,1,0:T(8,128)S(1)}, f32[3,3,1,2,136,128]{5,4,3,2,1,0:T(8,128)S(1)}, u32[]{:S(2)}, u32[]{:S(2)}) collective-permute-start(f32[3,3,1,2,136,128]{5,4,3,2,1,0:T(8,128)S(1)} %get-tuple-element.10), channel_id=1, source_target_pairs={{0,1},{1,2},{2,3},{3,4},{4,5},{5,6},{6,7},{7,8},{8,9},{9,10},{10,1... | collective-permute-start | bytes 3760136 | tf_op jit(solution)/shard_map/ppermute | solution.py:37
  124.8 19.4 %collective-permute-start.13 = (f32[3,3,1,2,136,128]{5,4,3,2,1,0:T(8,128)S(1)}, f32[3,3,1,2,136,128]{5,4,3,2,1,0:T(8,128)S(1)}, u32[]{:S(2)}, u32[]{:S(2)}) collective-permute-start(f32[3,3,1,2,136,128]{5,4,3,2,1,0:T(8,128)S(1)} %get-tuple-element.11), channel_id=1, source_target_pairs={{1,0},{2,1},{3,2},{4,3},{5,4},{6,5},{7,6},{8,7},{9,8},{10,9},{11,1... | collective-permute-start | bytes 3760136 | tf_op jit(solution)/shard_map/ppermute | solution.py:37
  144.6 8.6 %collective-permute-start.14 = (f32[3,1,1,2,136,128]{5,4,3,2,1,0:T(8,128)S(1)}, f32[3,1,1,2,136,128]{5,4,3,2,1,0:T(8,128)S(1)}, u32[]{:S(2)}, u32[]{:S(2)}) collective-permute-start(f32[3,1,1,2,136,128]{5,4,3,2,1,0:T(8,128)S(1)} %get-tuple-element.12), channel_id=1, source_target_pairs={{0,16},{16,32},{32,48},{48,64},{64,80},{80,96},{96,112},{112,128},... | collective-permute-start | bytes 1253384 | tf_op jit(solution)/shard_map/ppermute | solution.py:37
  148.2 8.8 %collective-permute-start.15 = (f32[3,1,1,2,136,128]{5,4,3,2,1,0:T(8,128)S(1)}, f32[3,1,1,2,136,128]{5,4,3,2,1,0:T(8,128)S(1)}, u32[]{:S(2)}, u32[]{:S(2)}) collective-permute-start(f32[3,1,1,2,136,128]{5,4,3,2,1,0:T(8,128)S(1)} %get-tuple-element.13), channel_id=1, source_target_pairs={{16,0},{32,16},{48,32},{64,48},{80,64},{96,80},{112,96},{128,112},... | collective-permute-start | bytes 1253384 | tf_op jit(solution)/shard_map/ppermute | solution.py:37
  157.1 16.7 %collective-permute-start.16 = (f32[1,1,1,2,136,128]{5,4,3,2,1,0:T(8,128)S(1)}, f32[1,1,1,2,136,128]{5,4,3,2,1,0:T(8,128)S(1)}, u32[]{:S(2)}, u32[]{:S(2)}) collective-permute-start(f32[1,1,1,2,136,128]{5,4,3,2,1,0:T(8,128)S(1)} %get-tuple-element.14), channel_id=1, source_target_pairs={{0,256},{256,512},{512,768},{1,257},{257,513},{513,769},{2,258},{2... | collective-permute-start | bytes 417800 | tf_op jit(solution)/shard_map/ppermute | solution.py:37
  171.8 34.1 %collective-permute-start.17 = (f32[1,1,1,2,136,128]{5,4,3,2,1,0:T(8,128)S(1)}, f32[1,1,1,2,136,128]{5,4,3,2,1,0:T(8,128)S(1)}, u32[]{:S(2)}, u32[]{:S(2)}) collective-permute-start(f32[1,1,1,2,136,128]{5,4,3,2,1,0:T(8,128)S(1)} %get-tuple-element.15), channel_id=1, source_target_pairs={{256,0},{512,256},{768,512},{257,1},{513,257},{769,513},{258,2},{5... | collective-permute-start | bytes 417800 | tf_op jit(solution)/shard_map/ppermute | solution.py:37

commit v2 on v1

--- a/solution.py
+++ b/solution.py
@@ -16,35 +16,6 @@
 ROWS = 136
 SCALING = (S * A) ** -0.5
 CHUNK = 32
-
-
-def extended(block, sides, width):
-    for axis, dim in sides:
-        count = lax.axis_size(axis)
-        forward = [(i, i + 1) for i in range(count - 1)]
-        backward = [(target, source) for source, target in forward]
-        low = lax.ppermute(
-            lax.slice_in_dim(block, block.shape[dim] - width, None, axis=dim), axis, forward
-        )
-        high = lax.ppermute(lax.slice_in_dim(block, 0, width, axis=dim), axis, backward)
-        block = jnp.concatenate([low, block, high], axis=dim)
-    return block
-
-
-def from_behind(block, axis, distance):
-    devices = range(lax.axis_size(axis))
-    route = [(i - distance, i) for i in devices if i - distance in devices]
-    return lax.ppermute(block, axis, route)
-
-
-def fold_plane(buffer, axis_dim, sender):
-    lower_plane = lax.slice_in_dim(buffer, 0, 1, axis=axis_dim)
-    middle_plane = lax.slice_in_dim(buffer, 1, 2, axis=axis_dim)
-    upper_plane = lax.slice_in_dim(buffer, 2, 3, axis=axis_dim)
-    result = middle_plane
-    for toward in (1, -1):
-        result = result + sender(upper_plane if toward == 1 else lower_plane, toward)
-    return result
 
 
 def pair_geometry(near, own, base, size):
@@ -148,6 +119,7 @@
                     own_acc[m, base : base + CHUNK, :] += force[m]
                     for k in range(0, CHUNK, 8):
                         column[m] = column[m] + force[m][k : k + 8]
+            contrib_force[pair + u] = jnp.zeros((8, A), jnp.float32)
             for m in range(3):
                 contrib_force[pair + u, m : m + 1, :] = -jnp.sum(column[m], axis=0, keepdims=True)
         return carry
@@ -157,11 +129,139 @@
         own_force[t, m : m + 1, :] = jnp.sum(jnp.transpose(own_acc[m]), axis=0, keepdims=True)
 
 
-def compute_kernel(
-    nbr, inverse, counts, rates, pos, near_pos, near_feat, mix, readout,
-    own_force, ghost,
-    own, basis, stack, sums, inv, grad, gbuf, own_acc, contrib, contrib_force,
+MESH = pl.DeviceIdType.MESH
+PLANE = [(dy, dz) for dy in (-1, 0, 1) for dz in (-1, 0, 1) if (dy, dz) != (0, 0)]
+
+
+def cell_of(dy, dz):
+    return (dy + 1) * 3 + dz + 1
+
+
+def step_kernel(
+    nbr, inverse, counts, rates, pos, feat, mix, readout,
+    forces, feature_grads,
+    near_feat, near_pos, own, basis, stack, sums, inv, grad, gbuf, own_acc, own_force, contrib, contrib_force,
+    plane_out, plane_in, far_out, far_in, pair_out, pair_in, far_sum, far_got, total,
+    feat_send, feat_recv, pos_send, pos_recv, grad_send, grad_recv,
 ):
+    x, y, z = lax.axis_index("gx"), lax.axis_index("gy"), lax.axis_index("gz")
+    ny, nz = lax.axis_size("gy"), lax.axis_size("gz")
+    toward = 1 - 2 * lax.rem(x, 2)
+    partner = (x + toward, y, z)
+    across = (x - toward, y, z)
+    has_far = (x - toward >= 0) & (x - toward < lax.axis_size("gx"))
+    pair_base = (toward + 1) * 9
+    far_base = (1 - toward) * 9
+    around = []
+    for dy, dz in PLANE:
+        exists = (y + dy >= 0) & (y + dy < ny) & (z + dz >= 0) & (z + dz < nz)
+        around.append((dy, dz, (x, y + dy, z + dz), exists))
+
+    zero_feat = jnp.zeros((T, A, C), jnp.bfloat16)
+    zero_pos = jnp.zeros((T, 3, A), jnp.float32)
+
+    def clear(c, carry):
+        near_feat[pl.ds(c * T, T)] = zero_feat
+        near_pos[pl.ds(c * T, T)] = zero_pos
+        return carry
+
+    lax.fori_loop(0, 27, clear, 0)
+
+    barrier = pltpu.get_barrier_semaphore()
+
+    @pl.when(has_far)
+    def _():
+        pl.semaphore_signal(barrier, inc=1, device_id=across, device_id_type=MESH)
+
+    for dy, dz, there, exists in around:
+        @pl.when(exists)
+        def _():
+            pl.semaphore_signal(barrier, inc=1, device_id=there, device_id_type=MESH)
+
+    pl.semaphore_signal(barrier, inc=1, device_id=partner, device_id_type=MESH)
+    rows_near = 3 - jnp.where(y == 0, 1, 0) - jnp.where(y == ny - 1, 1, 0)
+    columns_near = 3 - jnp.where(z == 0, 1, 0) - jnp.where(z == nz - 1, 1, 0)
+    pl.semaphore_wait(barrier, rows_near * columns_near + jnp.where(has_far, 1, 0))
+
+    def send_cell(feat_from, pos_from, cell, k, there):
+        rows = pl.ds(cell * T, T)
+        return (
+            pltpu.make_async_remote_copy(
+                feat_from, near_feat.at[rows], feat_send.at[k], feat_recv.at[k], device_id=there, device_id_type=MESH
+            ),
+            pltpu.make_async_remote_copy(
+                pos_from, near_pos.at[rows], pos_send.at[k], pos_recv.at[k], device_id=there, device_id_type=MESH
+            ),
+        )
+
+    def start(copies):
+        for copy in copies:
+            copy.start()
+
+    def arrive(copies):
+        for copy in copies:
+            copy.wait_recv()
+
+    def leave(copies):
+        for copy in copies:
+            copy.wait_send()
+
+    own_sends = []
+    far_sends = []
+    pair_sends = []
+    far_rows = pl.ds((far_base + 4) * T, T)
+    far_copy = send_cell(feat, pos, (pair_base + 4), 25, across)
+    for k, (dy, dz, there, exists) in enumerate(around):
+        own_sends.append(send_cell(feat, pos, 9 + cell_of(-dy, -dz), k, there))
+        far_sends.append(
+            send_cell(near_feat.at[far_rows], near_pos.at[far_rows], far_base + cell_of(-dy, -dz), 8 + k, there)
+        )
+        rows = pl.ds((9 + cell_of(dy, dz)) * T, T)
+        pair_sends.append(
+            send_cell(near_feat.at[rows], near_pos.at[rows], far_base + cell_of(dy, dz), 16 + k, partner)
+        )
+    centre_send = send_cell(feat, pos, far_base + 4, 24, partner)
+
+    @pl.when(has_far)
+    def _():
+        start(far_copy)
+
+    for k in range(8):
+        @pl.when(around[k][3])
+        def _():
+            start(own_sends[k])
+
+    start(centre_send)
+    near_feat[13 * T : 14 * T] = feat[...]
+    near_pos[13 * T : 14 * T] = pos[...]
+    for k in range(8):
+        @pl.when(around[k][3])
+        def _():
+            arrive(own_sends[7 - k])
+            start(pair_sends[k])
+
+    @pl.when(has_far)
+    def _():
+        arrive(far_copy)
+        for k in range(8):
+            @pl.when(around[k][3])
+            def _():
+                start(far_sends[k])
+
+    for k in range(8):
+        @pl.when(around[k][3])
+        def _():
+            arrive(pair_sends[k])
+
+    arrive(centre_send)
+
+    @pl.when(has_far)
+    def _():
+        for k in range(8):
+            @pl.when(around[k][3])
+            def _():
+                arrive(far_sends[7 - k])
+
     def one_tile(t, carry):
         tile_terms(
             t, nbr, counts, rates, pos, near_pos, near_feat, mix, readout,
@@ -171,23 +271,112 @@
 
     lax.fori_loop(0, T, one_tile, 0)
 
-    def gather(n, carry):
+    def collect(cell, u):
         block = jnp.zeros((A, C), jnp.float32)
         force = jnp.zeros((8, A), jnp.float32)
         for t in range(T):
-            s = inverse[t * NEAR + n]
+            s = inverse[t * NEAR + cell * T + u]
             pair = t * S + jnp.maximum(s, 0)
             block = block + jnp.where(s >= 0, contrib[pair], 0.0)
             force = force + jnp.where(s >= 0, contrib_force[pair], 0.0)
-        ghost[n, 0:A, :] = block
-        ghost[n, A:ROWS, :] = force
-        return carry
-
-    lax.fori_loop(0, NEAR, gather, 0)
-
-
-def compute(nbr, counts, rates, pos, near_pos, near_feat, mix, readout):
-    flat = nbr.reshape(T * S)
+        return block, force
+
+    def fill(ref, cell):
+        def one(u, carry):
+            block, force = collect(cell, u)
+            ref[u, 0:A, :] = block
+            ref[u, A:ROWS, :] = force
+            return carry
+
+        lax.fori_loop(0, T, one, 0)
+
+    def send_grad(from_ref, to_ref, k, there):
+        return pltpu.make_async_remote_copy(
+            from_ref, to_ref, grad_send.at[k], grad_recv.at[k], device_id=there, device_id_type=MESH
+        )
+
+    far_grads = [send_grad(far_out.at[k], far_in.at[k], k, around[k][2]) for k in range(8)]
+    own_grads = [send_grad(plane_out.at[k], plane_in.at[k], 8 + k, around[k][2]) for k in range(8)]
+    pair_grads = send_grad(pair_out, pair_in, 16, partner)
+    far_grad = send_grad(far_sum, far_got, 17, across)
+
+    @pl.when(has_far)
+    def _():
+        for k, (dy, dz, there, exists) in enumerate(around):
+            @pl.when(exists)
+            def _():
+                fill(far_out.at[k], far_base + cell_of(dy, dz))
+                far_grads[k].start()
+        fill(far_sum, far_base + 4)
+
+    def pair_cell(c, carry):
+        fill(pair_out.at[c], pair_base + c)
+        return carry
+
+    lax.fori_loop(0, 9, pair_cell, 0)
+    pair_grads.start()
+
+    @pl.when(has_far)
+    def _():
+        for k in range(8):
+            @pl.when(around[k][3])
+            def _():
+                far_grads[7 - k].wait_recv()
+                far_sum[...] += far_in[7 - k]
+        far_grad.start()
+
+    fill(total, 13)
+    pair_grads.wait_recv()
+    for k, (dy, dz, there, exists) in enumerate(around):
+        @pl.when(exists)
+        def _():
+            fill(plane_out.at[k], 9 + cell_of(dy, dz))
+            plane_out[k] += pair_in[cell_of(dy, dz)]
+            own_grads[k].start()
+
+    total[...] += pair_in[4]
+    for k in range(8):
+        @pl.when(around[k][3])
+        def _():
+            own_grads[7 - k].wait_recv()
+            total[...] += plane_in[7 - k]
+
+    @pl.when(has_far)
+    def _():
+        far_grad.wait_recv()
+        total[...] += far_got[...]
+
+    for t in range(T):
+        valid = lax.broadcasted_iota(jnp.int32, (A, C), 0) < counts[t]
+        feature_grads[t] = jnp.where(valid, total[t, 0:A, :], 0.0)
+        forces[t] = own_force[t] + total[t, A : A + 3, :]
+
+    @pl.when(has_far)
+    def _():
+        leave(far_copy)
+        far_grad.wait_send()
+        for k in range(8):
+            @pl.when(around[k][3])
+            def _():
+                leave(far_sends[k])
+                far_grads[k].wait_send()
+
+    for k in range(8):
+        @pl.when(around[k][3])
+        def _():
+            leave(own_sends[k])
+            leave(pair_sends[k])
+            own_grads[k].wait_send()
+
+    leave(centre_send)
+    pair_grads.wait_send()
+
+
+def body(positions, features, counts, neighbours, mix_weight, readout, radial_rates):
+    own_counts = counts.reshape(T)
+    is_valid = lax.broadcasted_iota(jnp.int32, (T, A, C), 1) < own_counts[:, None, None]
+    masked = jnp.where(is_valid, features.reshape(T, A, C), jnp.zeros((), jnp.bfloat16))
+    nbr = neighbours.reshape(T, S)
     where = jnp.where(
         nbr[:, :, None] == lax.broadcasted_iota(jnp.int32, (T, S, NEAR), 2),
         lax.broadcasted_iota(jnp.int32, (T, S, NEAR), 1),
@@ -196,15 +385,18 @@
     inverse = jnp.max(where, axis=1).reshape(T * NEAR)
     smem = pl.BlockSpec(memory_space=pltpu.SMEM)
     vmem = pl.BlockSpec(memory_space=pltpu.VMEM)
-    return pl.pallas_call(
-        compute_kernel,
+    cell = (T, ROWS, C)
+    forces, feature_grads = pl.pallas_call(
+        step_kernel,
         out_shape=(
             jax.ShapeDtypeStruct((T, 3, A), jnp.float32),
-            jax.ShapeDtypeStruct((NEAR, ROWS, C), jnp.float32),
+            jax.ShapeDtypeStruct((T, A, C), jnp.float32),
         ),
-        in_specs=[smem] * 4 + [vmem] * 5,
+        in_specs=[smem] * 4 + [vmem] * 4,
         out_specs=(vmem, vmem),
         scratch_shapes=[
+            pltpu.VMEM((NEAR, A, C), jnp.bfloat16),
+            pltpu.VMEM((NEAR, 3, A), jnp.float32),
             pltpu.VMEM((3, A, A), jnp.float32),
             pltpu.VMEM((4 * R * A, S * A), jnp.bfloat16),
             pltpu.VMEM((S * A, C), jnp.bfloat16),
@@ -213,36 +405,29 @@
             pltpu.VMEM((4 * R * A, C), jnp.bfloat16),
             pltpu.VMEM((4 * R * A, 2 * A), jnp.float32),
             pltpu.VMEM((3, A, A), jnp.float32),
+            pltpu.VMEM((T, 3, A), jnp.float32),
             pltpu.VMEM((T * S, A, C), jnp.float32),
             pltpu.VMEM((T * S, 8, A), jnp.float32),
+            pltpu.VMEM((8, *cell), jnp.float32),
+            pltpu.VMEM((8, *cell), jnp.float32),
+            pltpu.VMEM((8, *cell), jnp.float32),
+            pltpu.VMEM((8, *cell), jnp.float32),
+            pltpu.VMEM((9, *cell), jnp.float32),
+            pltpu.VMEM((9, *cell), jnp.float32),
+            pltpu.VMEM(cell, jnp.float32),
+            pltpu.VMEM(cell, jnp.float32),
+            pltpu.VMEM(cell, jnp.float32),
+            pltpu.SemaphoreType.DMA((26,)),
+            pltpu.SemaphoreType.DMA((26,)),
+            pltpu.SemaphoreType.DMA((26,)),
+            pltpu.SemaphoreType.DMA((26,)),
+            pltpu.SemaphoreType.DMA((18,)),
+            pltpu.SemaphoreType.DMA((18,)),
         ],
-        compiler_params=pltpu.CompilerParams(vmem_limit_bytes=48 * 1024 * 1024),
-    )(flat, inverse, counts, rates, pos, near_pos, near_feat, mix, readout)
-
-
-def body(positions, features, counts, neighbours, mix_weight, readout, radial_rates):
-    own_counts = counts.reshape(T)
-    is_valid = lax.broadcasted_iota(jnp.int32, (T, A), 1) < own_counts[:, None]
-    masked = jnp.where(is_valid.reshape(1, 1, 1, T, A, 1), features, jnp.zeros((), jnp.bfloat16))
-    near_points = extended(positions, (("gx", 0), ("gy", 1), ("gz", 2)), 1)
-    near_features = extended(masked, (("gx", 0), ("gy", 1), ("gz", 2)), 1)
-    own_force, ghost = compute(
-        neighbours.reshape(T, S),
-        own_counts,
-        radial_rates,
-        positions.reshape(T, 3, A),
-        near_points.reshape(NEAR, 3, A),
-        near_features.reshape(NEAR, A, C),
-        mix_weight,
-        readout.reshape(1, C),
-    )
-    buffer = ghost.reshape(3, 3, 3, T, ROWS, C)
-    buffer = fold_plane(buffer, 2, lambda values, toward: from_behind(values, "gz", toward))
-    buffer = fold_plane(buffer, 1, lambda values, toward: from_behind(values, "gy", toward))
-    buffer = fold_plane(buffer, 0, lambda values, toward: from_behind(values, "gx", toward))
-    center = buffer.reshape(T, ROWS, C)
-    forces = own_force + center[:, A : A + 3, :]
-    feature_grads = jnp.where(is_valid[:, :, None], center[:, :A, :], 0.0)
+        compiler_params=pltpu.CompilerParams(
+            collective_id=0, has_side_effects=True, vmem_limit_bytes=56 * 1024 * 1024
+        ),
+    )(nbr.reshape(T * S), inverse, own_counts, radial_rates, positions.reshape(T, 3, A), masked, mix_weight, readout.reshape(1, C))
     return (
         forces.reshape(1, 1, 1, T, 3, A),
         feature_grads.reshape(1, 1, 1, T, A, C),

time: 210 us -> 108 us (0.51); the launches traced: 207 us -> 108 us
  starting transfers between devices: 109 us -> 0 us
  Pallas kernels: 17.4 us -> 99.6 us
  waiting for transfers between devices: 74.4 us -> 0 us
  local copies, waits for them, and re-layouts: 2.37 us -> 5.94 us
    ppermute x18 -> x0, starting transfers between devices: 109 us -> none  [the longest x6 63.7 us: extended(): lax.ppermute(lax.slice_in_dim(block, block.shape[dim] - width, None, axis...]
    pallas_call x1, Pallas kernels: 17.4 us -> 99.6 us  [body(): pl.pallas_call(step_kernel, out_shape=(jax.ShapeDtypeStruct((T, 3, A), jn...]
    ppermute x18 -> x0, waiting for transfers between devices: 74.4 us -> none  [the longest x6 53.5 us: from_behind(): return lax.ppermute(block, axis, route)]
    unnamed x16 -> x11, local copies, waits for them, and re-layouts: 1.93 us -> 4.74 us
  transfers between devices with their start and end apart: 18 -> 0, of which waited for: 11 -> 0; matrix products, arithmetic and copies ran while one was open for 1% -> 0% of each run, Pallas kernels for 0% -> 0%
where the time goes in v2:
time: 108 us
  Pallas kernels  99.6 us (92%)
  local copies, waits for them, and re-layouts  5.94 us (6%)
  other arithmetic  1.64 us (2%)
    pallas_call x1, Pallas kernels, body(): pl.pallas_call(step_kernel, out_shape=(jax.ShapeDtypeStruct((T, 3, A), jn...  99.6 us
    unnamed x11, local copies, waits for them, and re-layouts  4.74 us

profile of v2, /device:TPU:25, one launch (start us, length us, event | category | flops | bytes accessed | tf_op | source)
XLA Modules:
  0.0 107.9 jit_solution(7405862693392026152)
XLA Ops:
  0.6 0.0 copy-start.3
  0.6 0.7 copy-done.3
  1.3 0.0 copy-start.1
  1.3 0.6 reshape_reshape.3.nbr
  1.9 0.1 select_reduce_fusion
  2.0 0.6 reshape.27.inverse
  2.6 0.0 copy-done.1
  2.6 0.6 copy.14
  3.2 0.0 copy-start.2
  3.2 0.7 copy-done.2
  3.9 1.5 %fusion.feat = bf16[2,128,128]{2,1,0:T(8,128)(2,1)} fusion(bf16[1,1,1,2,128,128]{5,4,3,2,1,0:T(8,128)(2,1)} %param.8, s32[2]{0:T(128)S(1)} %bitcast.14), kind=kLoop, calls=%fused_computation.1 | loop fusion | flops 65536 | bytes 131080 | tf_op jit(solution)/shard_map/jit(_where)/select_n | solution.py:378
  5.4 99.6 %shard_map.86 = (f32[2,3,128]{2,1,0:T(4,128)}, f32[2,128,128]{2,1,0:T(8,128)}) custom-call(s32[16]{0:T(128)} %reshape_reshape.3.nbr, s32[108]{0:T(128)} %reshape.27.inverse, s32[2]{0:T(128)} %bitcast.13, f32[4]{0:T(128)} %rates.1, f32[2,3,128]{2,1,0:T(4,128)} %bitcast.11, bf16[2,128,128]{2,1,0:T(8,128)(2,1)} %fusion.feat, bf16[1024,128]{1,0:T(8,128)(2,1)} %mix.1, ...), custom_call_target="tpu_custom_call" | custom-call | tf_op jit(solution)/shard_map/pallas_call | solution.py:389
  105.1 0.0 copy-start
  105.1 0.7 copy-done
  105.7 0.6 copy.12
  106.3 1.6 %copy.16 = f32[1,1,1,2,128,128]{5,4,3,2,1,0:T(8,128)} copy(f32[1,1,1,2,128,128]{5,4,3,2,1,0:T(8,128)} %bitcast.10) | data formatting | bytes 262144
Async XLA Ops:
  0.6 0.7 copy-start.3
  1.3 1.3 %copy-start.1 = (f32[1,1,1,2,3,128]{5,3,4,2,1,0:T(2,128)S(1)}, f32[1,1,1,2,3,128]{5,3,4,2,1,0:T(2,128)}, u32[]{:S(2)}) copy-start(f32[1,1,1,2,3,128]{5,3,4,2,1,0:T(2,128)} %param.7) | copy-start | bytes 9220
  3.2 0.7 copy-start.2
  105.1 0.7 copy-start

commit v3 on v2

v3 whole, which is shorter than its diff:
```python
import functools

import jax
import jax.numpy as jnp
from jax import lax
from jax.experimental import pallas as pl
from jax.experimental.pallas import tpu as pltpu
from jax.sharding import PartitionSpec as P

A = 128
C = 128
R = 4
S = 8
T = 2
NEAR = 27 * T
ROWS = 136
SCALING = (S * A) ** -0.5
CHUNK = 32


def pair_geometry(near, own, t, base, size):
    offset = [near[m : m + 1, :] - own[t, m, pl.ds(base, size), :] for m in range(3)]
    square = offset[0] * offset[0] + offset[1] * offset[1] + offset[2] * offset[2]
    return offset, square


def tile_gradients(
    t, nbr, counts, rates, pos, near_pos, near_feat, mix, readout, own, basis, stack, sums, inv, grad, contrib
):
    for m in range(3):
        own[t, m] = jnp.transpose(jnp.broadcast_to(pos[t, m : m + 1, :], (A, A)))

    def build(s, carry):
        n = nbr[t * S + s]
        source = jnp.maximum(n, 0)
        near = near_pos[source]
        lanes = pl.ds(pl.multiple_of(s * A, A), A)
        tile = near_feat[source]
        stack[t, lanes, :] = jnp.where(n >= 0, tile, jnp.zeros_like(tile))
        for base in range(0, A, CHUNK):
            offset, square = pair_geometry(near, own, t, base, CHUNK)
            for r in range(R):
                g = jnp.exp(-rates[r] * square)
                for m in range(4):
                    value = g if m == 0 else g * offset[m - 1]
                    row = (r * 4 + m) * A + base
                    basis[t, row : row + CHUNK, lanes] = value.astype(jnp.bfloat16)
        return carry

    lax.fori_loop(0, S, build, 0)

    def forward(k, carry):
        rows = pl.ds(pl.multiple_of(k * 4 * A, 4 * A), 4 * A)
        sums[rows, :] = jnp.dot(basis[t, rows, :], stack[t], preferred_element_type=jnp.float32) * SCALING
        return carry

    lax.fori_loop(0, R, forward, 0)

    for r in range(R):
        base = r * 4 * A
        inv[:, r * C : (r + 1) * C] = sums[base : base + A, :].astype(jnp.bfloat16)
        total = jnp.zeros((A, C), jnp.float32)
        for m in range(1, 4):
            part = sums[base + m * A : base + (m + 1) * A, :]
            total = total + part * part
        inv[:, (R + r) * C : (R + r + 1) * C] = total.astype(jnp.bfloat16)
    preact = jnp.dot(inv[...], mix[...], preferred_element_type=jnp.float32)
    sigmoid = 1.0 / (1.0 + jnp.exp(-preact))
    valid = lax.broadcasted_iota(jnp.int32, (A, C), 0) < counts[t]
    grad_pre = readout[...] * sigmoid * (1.0 + preact * (1.0 - sigmoid))
    grad_pre = jnp.where(valid, grad_pre, 0.0).astype(jnp.bfloat16)
    for r in range(R):
        base = r * 4 * A
        for half in range(2):
            k = half * R + r
            gi = lax.dot_general(
                grad_pre, mix[k * C : (k + 1) * C, :], (((1,), (1,)), ((), ())),
                preferred_element_type=jnp.float32,
            )
            if half == 0:
                grad[t, base : base + A, :] = (gi * SCALING).astype(jnp.bfloat16)
            else:
                for m in range(1, 4):
                    rows = slice(base + m * A, base + (m + 1) * A)
                    grad[t, rows, :] = (2.0 * sums[rows, :] * gi * SCALING).astype(jnp.bfloat16)

    def spread(p, carry):
        wide = pl.ds(pl.multiple_of(p * 2 * A, 2 * A), 2 * A)
        near_grad = lax.dot_general(
            basis[t, :, wide], grad[t], (((0,), (0,)), ((), ())), preferred_element_type=jnp.float32
        )
        pair = t * S + p * 2
        contrib[pair] = near_grad[:A]
        contrib[pair + 1] = near_grad[A:]
        return carry

    lax.fori_loop(0, S // 2, spread, 0)


def tile_forces(t, nbr, rates, near_pos, own, stack, grad, gbuf, own_acc, contrib_force, own_force):
    for m in range(3):
        own_acc[m] = jnp.zeros((A, A), jnp.float32)

    def backward(p, carry):
        wide = pl.ds(pl.multiple_of(p * 2 * A, 2 * A), 2 * A)
        pair = t * S + p * 2
        gbuf[...] = lax.dot_general(
            grad[t], stack[t, wide, :], (((1,), (1,)), ((), ())), preferred_element_type=jnp.float32
        )
        for u in range(2):
            near = near_pos[jnp.maximum(nbr[pair + u], 0)]
            cols = slice(u * A, (u + 1) * A)
            column = [jnp.zeros((8, A), jnp.float32) for _ in range(3)]
            for base in range(0, A, CHUNK):
                offset, square = pair_geometry(near, own, t, base, CHUNK)
                force = [None] * 3
                pull = None
                for r in range(R):
                    g = jnp.exp(-rates[r] * square)
                    gb = [gbuf[(r * 4 + m) * A + base : (r * 4 + m) * A + base + CHUNK, cols] for m in range(4)]
                    inner = gb[0] + gb[1] * offset[0] + gb[2] * offset[1] + gb[3] * offset[2]
                    term = (2.0 * rates[r]) * g * inner
                    pull = term if pull is None else pull + term
                    for m in range(3):
                        part = g * gb[m + 1]
                        force[m] = part if force[m] is None else force[m] + part
                for m in range(3):
                    force[m] = force[m] - offset[m] * pull
                    own_acc[m, base : base + CHUNK, :] += force[m]
                    for k in range(0, CHUNK, 8):
                        column[m] = column[m] + force[m][k : k + 8]
            contrib_force[pair + u] = jnp.zeros((8, A), jnp.float32)
            for m in range(3):
                contrib_force[pair + u, m : m + 1, :] = -jnp.sum(column[m], axis=0, keepdims=True)
        return carry

    lax.fori_loop(0, S // 2, backward, 0)
    for m in range(3):
        own_force[t, m : m + 1, :] = jnp.sum(jnp.transpose(own_acc[m]), axis=0, keepdims=True)


MESH = pl.DeviceIdType.MESH
PLANE = [(dy, dz) for dy in (-1, 0, 1) for dz in (-1, 0, 1) if (dy, dz) != (0, 0)]


def cell_of(dy, dz):
    return (dy + 1) * 3 + dz + 1


def step_kernel(
    nbr, counts, rates, pos, feat, mix, readout,
    forces, feature_grads,
    inverse, near_feat, near_pos, relay_feat, relay_pos,
    own, basis, stack, sums, inv, grad, gbuf, own_acc, own_force, contrib, contrib_force,
    feat_send, feat_recv, pos_send, pos_recv, *fold_refs,
):
    x, y, z = lax.axis_index("gx"), lax.axis_index("gy"), lax.axis_index("gz")
    ny, nz = lax.axis_size("gy"), lax.axis_size("gz")
    toward = 1 - 2 * lax.rem(x, 2)
    partner = (x + toward, y, z)
    has_far = (x - toward >= 0) & (x - toward < lax.axis_size("gx"))
    no_far = (x - toward < 0) | (x - toward >= lax.axis_size("gx"))
    pair_base = (toward + 1) * 9
    far_base = (1 - toward) * 9
    around = []
    for dy, dz in PLANE:
        exists = (y + dy >= 0) & (y + dy < ny) & (z + dz >= 0) & (z + dz < nz)
        around.append((dy, dz, (x, y + dy, z + dz), exists))

    place = jnp.where(x == 2, ny, 0) + y

    def ring(step):
        spot = lax.rem(place + step + 2 * ny, 2 * ny)
        side = spot // ny
        return (1 + side, lax.rem(spot, ny), z), (1 - side) * 18

    up, down = ring(1)[0], ring(-1)[0]
    (ahead, ahead_base), (behind, behind_base) = ring(ny - 1), ring(1 - ny)

    barrier = pltpu.get_barrier_semaphore()

    @pl.when(has_far)
    def _():
        for there in (ahead, behind):
            pl.semaphore_signal(barrier, inc=1, device_id=there, device_id_type=MESH)

        @pl.when(y == ny - 1)
        def _():
            pl.semaphore_signal(barrier, inc=1, device_id=up, device_id_type=MESH)

        @pl.when(y == 0)
        def _():
            pl.semaphore_signal(barrier, inc=1, device_id=down, device_id_type=MESH)

    for dy, dz, there, exists in around:
        @pl.when(exists)
        def _():
            pl.semaphore_signal(barrier, inc=1, device_id=there, device_id_type=MESH)

    pl.semaphore_signal(barrier, inc=1, device_id=partner, device_id_type=MESH)

    for t in range(T):
        valid = lax.broadcasted_iota(jnp.int32, (A, C), 0) < counts[t]
        near_feat[13 * T + t] = jnp.where(valid, feat[t].astype(jnp.float32), 0.0).astype(jnp.bfloat16)
    near_pos[13 * T : 14 * T] = pos[...]

    def clear(c):
        near_feat[pl.ds(c * T, T)] = jnp.zeros((T, A, C), jnp.bfloat16)
        near_pos[pl.ds(c * T, T)] = jnp.zeros((T, 3, A), jnp.float32)

    for dy, dz in PLANE:
        @pl.when((y + dy < 0) | (y + dy >= ny) | (z + dz < 0) | (z + dz >= nz))
        def _():
            for first in (0, 9, 18):
                clear(first + cell_of(dy, dz))

    @pl.when(no_far)
    def _():
        def one(c, carry):
            clear(far_base + c)
            return carry

        lax.fori_loop(0, 9, one, 0)

    def invert(n, carry):
        for t in range(T):
            found = jnp.int32(-1)
            for slot in range(S):
                found = jnp.where(nbr[t * S + slot] == n, slot, found)
            inverse[t * NEAR + n] = found
        return carry

    lax.fori_loop(0, NEAR, invert, 0)

    rows_near = 3 - jnp.where(y == 0, 1, 0) - jnp.where(y == ny - 1, 1, 0)
    columns_near = 3 - jnp.where(z == 0, 1, 0) - jnp.where(z == nz - 1, 1, 0)
    ring_peers = 2 + jnp.where(y == 0, 1, 0) + jnp.where(y == ny - 1, 1, 0)
    pl.semaphore_wait(barrier, rows_near * columns_near + jnp.where(has_far, ring_peers, 0))

    def send_tiles(feat_from, pos_from, feat_to, pos_to, k, there):
        return (
            pltpu.make_async_remote_copy(
                feat_from, feat_to, feat_send.at[k], feat_recv.at[k], device_id=there, device_id_type=MESH
            ),
            pltpu.make_async_remote_copy(
                pos_from, pos_to, pos_send.at[k], pos_recv.at[k], device_id=there, device_id_type=MESH
            ),
        )

    def send_rows(source, target, k, there):
        return send_tiles(near_feat.at[source], near_pos.at[source], near_feat.at[target], near_pos.at[target], k, there)

    def start(copies):
        for copy in copies:
            copy.start()

    def arrive(copies):
        for copy in copies:
            copy.wait_recv()

    def leave(copies):
        for copy in copies:
            copy.wait_send()

    def cells(cell):
        return pl.ds(cell * T, T)

    own_sends, far_sends, pair_sends = [], [[], []], []
    for k, (dy, dz, there, exists) in enumerate(around):
        own_sends.append(send_rows(cells(13), cells(9 + cell_of(-dy, -dz)), k, there))
        for t in range(T):
            target = pl.ds((far_base + cell_of(-dy, -dz)) * T + t, 1)
            far_sends[t].append(send_rows(pl.ds((far_base + 4) * T + t, 1), target, 8 + 8 * t + k, there))
        pair_sends.append(send_rows(cells(9 + cell_of(dy, dz)), cells(far_base + cell_of(dy, dz)), 24 + k, partner))
    centre_send = send_rows(cells(13), cells(far_base + 4), 32, partner)
    hops, relays = [], []
    for t, (first, last, last_base) in enumerate(((up, ahead, ahead_base), (down, behind, behind_base))):
        slot, source = pl.ds(t, 1), pl.ds(13 * T + t, 1)
        hops.append(
            send_tiles(near_feat.at[source], near_pos.at[source], relay_feat.at[slot], relay_pos.at[slot], 33 + t, first)
        )
        target = pl.ds((last_base + 4) * T + t, 1)
        relays.append(
            send_tiles(relay_feat.at[slot], relay_pos.at[slot], near_feat.at[target], near_pos.at[target], 35 + t, last)
        )

    @pl.when(has_far)
    def _():
        for t in range(T):
            start(hops[t])
        for t in range(T):
            arrive(hops[t])
            start(relays[t])

    for k in range(8):
        @pl.when(around[k][3])
        def _():
            start(own_sends[k])

    start(centre_send)
    for k in range(8):
        @pl.when(around[k][3])
        def _():
            arrive(own_sends[7 - k])
            start(pair_sends[k])

    for k in range(8):
        @pl.when(around[k][3])
        def _():
            arrive(pair_sends[k])

    arrive(centre_send)

    @pl.when(has_far)
    def _():
        for t in range(T):
            arrive(relays[t])
            for k in range(8):
                @pl.when(around[k][3])
                def _():
                    start(far_sends[t][k])
        for t in range(T):
            for k in range(8):
                @pl.when(around[k][3])
                def _():
                    arrive(far_sends[t][7 - k])

    def gradients(t, carry):
        tile_gradients(
            t, nbr, counts, rates, pos, near_pos, near_feat, mix, readout,
            own, basis, stack, sums, inv, grad, contrib,
        )
        return carry

    lax.fori_loop(0, T, gradients, 0)

    folds = [
        Fold(refs, source, inverse, around, (up, down), (ahead, behind), partner, (x, y, z), (ny, nz), (pair_base, far_base))
        for refs, source in ((fold_refs[:13], contrib), (fold_refs[13:], contrib_force))
    ]
    feature, push = folds

    def act(tile):
        tile_forces(tile, nbr, rates, near_pos, own, stack, grad, gbuf, own_acc, contrib_force, own_force)

    @pl.when(has_far)
    def _():
        feature.send_far_column()

    feature.send_pair_column()
    act(0)

    @pl.when(has_far)
    def _():
        feature.sum_far_column()

    act(1)

    @pl.when(has_far)
    def _():
        feature.relay()
        push.send_far_column()

    push.send_pair_column()
    feature.send_sides()

    @pl.when(has_far)
    def _():
        push.sum_far_column()

    push.send_sides()

    @pl.when(has_far)
    def _():
        push.relay()

    feature.send_rows()
    push.send_rows()
    feature.finish()
    push.finish()

    @pl.when(has_far)
    def _():
        push.finish_far()
        feature.finish_far()

    for t in range(T):
        valid = lax.broadcasted_iota(jnp.int32, (A, C), 0) < counts[t]
        feature_grads[t] = jnp.where(valid, feature.mid[1, t], 0.0)
        forces[t] = own_force[t] + push.mid[1, t, 0:3, :]

    @pl.when(has_far)
    def _():
        for t in range(T):
            leave(hops[t])
            leave(relays[t])
        for k in range(8):
            @pl.when(around[k][3])
            def _():
                for t in range(T):
                    leave(far_sends[t][k])

    for k in range(8):
        @pl.when(around[k][3])
        def _():
            leave(own_sends[k])
            leave(pair_sends[k])

    leave(centre_send)
    for fold in folds:
        fold.leave(has_far)


class Fold:
    def __init__(self, refs, source, inverse, around, near_ring, far_ring, partner, me, sizes, bases):
        (
            self.far_out, self.far_in, self.far_sum, self.passing, self.far_got,
            self.pair_out, self.pair_in, self.side_out, self.side_in, self.mid, self.row_in, send, recv,
        ) = refs
        self.source, self.inverse, self.around = source, inverse, around
        self.pair_base, self.far_base = bases
        (x, y, z), (ny, nz) = me, sizes

        def copy(from_ref, to_ref, k, there):
            return pltpu.make_async_remote_copy(
                from_ref, to_ref, send.at[k], recv.at[k], device_id=there, device_id_type=MESH
            )

        self.far = [copy(self.far_out.at[k], self.far_in.at[k], k, around[k][2]) for k in range(8)]
        self.pair = copy(self.pair_out, self.pair_in, 8, partner)
        self.side = [copy(self.side_out.at[d], self.side_in.at[d], 9 + d, (x, y, z + 2 * d - 1)) for d in range(2)]
        self.side_exists = [z > 0, z < nz - 1]
        self.row = [copy(self.mid.at[2 * d], self.row_in.at[d], 11 + d, (x, y + 2 * d - 1, z)) for d in range(2)]
        self.row_exists = [y > 0, y < ny - 1]
        self.hop = [copy(self.far_sum.at[t], self.passing.at[t], 13 + t, near_ring[t]) for t in range(T)]
        self.last = [copy(self.passing.at[t], self.far_got.at[t], 15 + t, far_ring[t]) for t in range(T)]

    def fill(self, ref, cell, extra=None):
        def one(u, carry):
            block = None
            for t in range(T):
                s = self.inverse[t * NEAR + cell * T + u]
                part = jnp.where(s >= 0, self.source[t * S + jnp.maximum(s, 0)], 0.0)
                block = part if block is None else block + part
            if extra is not None:
                block = block + extra[u]
            ref[u] = block
            return carry

        lax.fori_loop(0, T, one, 0)

    def send_far_column(self):
        for k, (dy, dz, there, exists) in enumerate(self.around):
            @pl.when(exists)
            def _():
                self.fill(self.far_out.at[k], self.far_base + cell_of(dy, dz))
                self.far[k].start()
        self.fill(self.far_sum, self.far_base + 4)

    def send_pair_column(self):
        def one(c, carry):
            self.fill(self.pair_out.at[c], self.pair_base + c)
            return carry

        lax.fori_loop(0, 9, one, 0)
        self.pair.start()

    def sum_far_column(self):
        for k in range(8):
            @pl.when(self.around[k][3])
            def _():
                self.far[7 - k].wait_recv()
                self.far_sum[...] += self.far_in[7 - k]
        for t in range(T):
            self.hop[t].start()

    def relay(self):
        for t in range(T):
            self.hop[t].wait_recv()
            self.last[t].start()

    def send_sides(self):
        self.pair.wait_recv()
        for d in range(2):
            @pl.when(self.side_exists[d])
            def _():
                for row in range(3):
                    c = row * 3 + 2 * d
                    self.fill(self.side_out.at[d, row], 9 + c, self.pair_in.at[c])
                self.side[d].start()
        for row in range(3):
            c = row * 3 + 1
            self.fill(self.mid.at[row], 9 + c, self.pair_in.at[c])

    def send_rows(self):
        for d in range(2):
            @pl.when(self.side_exists[d])
            def _():
                self.side[1 - d].wait_recv()
                for row in range(3):
                    self.mid[row] += self.side_in[1 - d, row]
        for d in range(2):
            @pl.when(self.row_exists[d])
            def _():
                self.row[d].start()

    def finish(self):
        for d in range(2):
            @pl.when(self.row_exists[d])
            def _():
                self.row[1 - d].wait_recv()
                self.mid[1] += self.row_in[1 - d]

    def finish_far(self):
        for t in range(T):
            self.last[t].wait_recv()
            self.mid[1, t] += self.far_got[t]

    def leave(self, has_far):
        @pl.when(has_far)
        def _():
            for k in range(8):
                @pl.when(self.around[k][3])
                def _():
                    self.far[k].wait_send()
            for t in range(T):
                self.hop[t].wait_send()
                self.last[t].wait_send()

        self.pair.wait_send()
        for d in range(2):
            @pl.when(self.side_exists[d])
            def _():
                self.side[d].wait_send()

            @pl.when(self.row_exists[d])
            def _():
                self.row[d].wait_send()


def fold_scratch(tile):
    shapes = [(8, T), (8, T), (T,), (T,), (T,), (9, T), (9, T), (2, 3, T), (2, 3, T), (3, T), (2, T)]
    return [pltpu.VMEM((*lead, *tile), jnp.float32) for lead in shapes] + [pltpu.SemaphoreType.DMA((17,))] * 2


def body(positions, features, counts, neighbours, mix_weight, readout, radial_rates):
    smem = pl.BlockSpec(memory_space=pltpu.SMEM)
    vmem = pl.BlockSpec(memory_space=pltpu.VMEM)
    forces, feature_grads = pl.pallas_call(
        step_kernel,
        out_shape=(
            jax.ShapeDtypeStruct((T, 3, A), jnp.float32),
            jax.ShapeDtypeStruct((T, A, C), jnp.float32),
        ),
        in_specs=[smem] * 3 + [vmem] * 4,
        out_specs=(vmem, vmem),
        scratch_shapes=[
            pltpu.SMEM((T * NEAR,), jnp.int32),
            pltpu.VMEM((NEAR, A, C), jnp.bfloat16),
            pltpu.VMEM((NEAR, 3, A), jnp.float32),
            pltpu.VMEM((T, A, C), jnp.bfloat16),
            pltpu.VMEM((T, 3, A), jnp.float32),
            pltpu.VMEM((T, 3, A, A), jnp.float32),
            pltpu.VMEM((T, 4 * R * A, S * A), jnp.bfloat16),
            pltpu.VMEM((T, S * A, C), jnp.bfloat16),
            pltpu.VMEM((4 * R * A, C), jnp.float32),
            pltpu.VMEM((A, 2 * R * C), jnp.bfloat16),
            pltpu.VMEM((T, 4 * R * A, C), jnp.bfloat16),
            pltpu.VMEM((4 * R * A, 2 * A), jnp.float32),
            pltpu.VMEM((3, A, A), jnp.float32),
            pltpu.VMEM((T, 3, A), jnp.float32),
            pltpu.VMEM((T * S, A, C), jnp.float32),
            pltpu.VMEM((T * S, 8, A), jnp.float32),
            pltpu.SemaphoreType.DMA((37,)),
            pltpu.SemaphoreType.DMA((37,)),
            pltpu.SemaphoreType.DMA((37,)),
            pltpu.SemaphoreType.DMA((37,)),
            *fold_scratch((A, C)),
            *fold_scratch((8, A)),
        ],
        compiler_params=pltpu.CompilerParams(
            collective_id=0, has_side_effects=True, vmem_limit_bytes=56 * 1024 * 1024
        ),
    )(
        neighbours.reshape(T * S), counts.reshape(T), radial_rates, positions.reshape(T, 3, A),
        features.reshape(T, A, C), mix_weight, readout.reshape(1, C),
    )
    return (
        forces.reshape(1, 1, 1, T, 3, A),
        feature_grads.reshape(1, 1, 1, T, A, C),
    )


def solution(mesh):
    cell = ("gx", "gy", "gz")
    in_specs = (
        P(*cell, None, None, None),
        P(*cell, None, None, None),
        P(*cell, None),
        P(*cell, None, None),
        P(),
        P(),
        P(),
    )
    out_specs = (P(*cell, None, None, None), P(*cell, None, None, None))
    return jax.shard_map(body, mesh=mesh, in_specs=in_specs, out_specs=out_specs, check_vma=False)
```

time: 108 us -> 115 us (1.065); the launches traced: 108 us -> 113 us
  Pallas kernels: 99.6 us -> 108 us
  other arithmetic: 1.64 us -> 0 us
  local copies, waits for them, and re-layouts: 5.94 us -> 4.66 us
    pallas_call x1, Pallas kernels: 99.6 us -> 108 us  [body(): pl.pallas_call(step_kernel, out_shape=(jax.ShapeDtypeStruct((T, 3, A), jn...]
    select_n x1 -> x0, other arithmetic: 1.55 us -> none  [body(): jnp.where(is_valid, features.reshape(T, A, C), jnp.zeros((), jnp.bfloat16))]
    unnamed x11 -> x9, local copies, waits for them, and re-layouts: 4.74 us -> 4.07 us
where the time goes in v3:
time: 115 us; the launch traced here: 113 us
  Pallas kernels  108 us (94%)
  local copies, waits for them, and re-layouts  4.66 us (4%)
    pallas_call x1, Pallas kernels, body(): pl.pallas_call(step_kernel, out_shape=(jax.ShapeDtypeStruct((T, 3, A), jn...  108 us
    unnamed x9, local copies, waits for them, and re-layouts  4.07 us

profile of v3, /device:TPU:25, one launch (start us, length us, event | category | flops | bytes accessed | tf_op | source)
XLA Modules:
  0.0 113.4 jit_solution(11695263677950781724)
XLA Ops:
  0.6 0.0 copy-start.2
  0.6 0.0 copy-start.1
  0.6 0.7 copy-done.2
  1.3 0.6 reshape.25.nbr
  1.9 0.0 copy-done.1
  1.9 0.6 copy.12
  2.5 108.1 %shard_map.86 = (f32[2,3,128]{2,1,0:T(4,128)}, f32[2,128,128]{2,1,0:T(8,128)}) custom-call(s32[16]{0:T(128)} %reshape.25.nbr, s32[2]{0:T(128)} %bitcast.12, f32[4]{0:T(128)} %rates.1, f32[2,3,128]{2,1,0:T(4,128)} %bitcast.10, bf16[2,128,128]{2,1,0:T(8,128)(2,1)} %bitcast.9, bf16[1024,128]{1,0:T(8,128)(2,1)} %mix.1, f32[1,128]{1,0:T(1,128)} %bitcast.13), custom_call_target="tpu_custom_call" | custom-call | tf_op jit(solution)/shard_map/pallas_call | solution.py:549
  110.6 0.0 copy-start
  110.6 0.7 copy-done
  111.3 0.6 copy.10
  111.9 1.6 %copy.14 = f32[1,1,1,2,128,128]{5,4,3,2,1,0:T(8,128)} copy(f32[1,1,1,2,128,128]{5,4,3,2,1,0:T(8,128)} %bitcast.8) | data formatting | bytes 262144
Async XLA Ops:
  0.6 0.7 copy-start.2
  0.6 1.3 %copy-start.1 = (f32[1,1,1,2,3,128]{5,3,4,2,1,0:T(2,128)S(1)}, f32[1,1,1,2,3,128]{5,3,4,2,1,0:T(2,128)}, u32[]{:S(2)}) copy-start(f32[1,1,1,2,3,128]{5,3,4,2,1,0:T(2,128)} %param.7) | copy-start | bytes 9220
  110.6 0.7 copy-start

commit v4 on v3

--- a/solution.py
+++ b/solution.py
@@ -24,9 +24,7 @@
     return offset, square
 
 
-def tile_gradients(
-    t, nbr, counts, rates, pos, near_pos, near_feat, mix, readout, own, basis, stack, sums, inv, grad, contrib
-):
+def tile_basis(t, nbr, rates, pos, near_pos, own, basis):
     for m in range(3):
         own[t, m] = jnp.transpose(jnp.broadcast_to(pos[t, m : m + 1, :], (A, A)))
 
@@ -35,8 +33,6 @@
         source = jnp.maximum(n, 0)
         near = near_pos[source]
         lanes = pl.ds(pl.multiple_of(s * A, A), A)
-        tile = near_feat[source]
-        stack[t, lanes, :] = jnp.where(n >= 0, tile, jnp.zeros_like(tile))
         for base in range(0, A, CHUNK):
             offset, square = pair_geometry(near, own, t, base, CHUNK)
             for r in range(R):
@@ -48,6 +44,13 @@
         return carry
 
     lax.fori_loop(0, S, build, 0)
+
+
+def tile_gradients(t, nbr, counts, near_feat, mix, readout, basis, stack, sums, inv, grad, contrib):
+    for s in range(S):
+        n = nbr[t * S + s]
+        tile = near_feat[jnp.maximum(n, 0)]
+        stack[t, s * A : (s + 1) * A, :] = jnp.where(n >= 0, tile, jnp.zeros_like(tile))
 
     def forward(k, carry):
         rows = pl.ds(pl.multiple_of(k * 4 * A, 4 * A), 4 * A)
@@ -150,7 +153,7 @@
 def step_kernel(
     nbr, counts, rates, pos, feat, mix, readout,
     forces, feature_grads,
-    inverse, near_feat, near_pos, relay_feat, relay_pos,
+    inverse, near_feat, near_pos,
     own, basis, stack, sums, inv, grad, gbuf, own_acc, own_force, contrib, contrib_force,
     feat_send, feat_recv, pos_send, pos_recv, *fold_refs,
 ):
@@ -167,30 +170,13 @@
         exists = (y + dy >= 0) & (y + dy < ny) & (z + dz >= 0) & (z + dz < nz)
         around.append((dy, dz, (x, y + dy, z + dz), exists))
 
-    place = jnp.where(x == 2, ny, 0) + y
-
-    def ring(step):
-        spot = lax.rem(place + step + 2 * ny, 2 * ny)
-        side = spot // ny
-        return (1 + side, lax.rem(spot, ny), z), (1 - side) * 18
-
-    up, down = ring(1)[0], ring(-1)[0]
-    (ahead, ahead_base), (behind, behind_base) = ring(ny - 1), ring(1 - ny)
+    across = (x - toward, y, z)
 
     barrier = pltpu.get_barrier_semaphore()
 
     @pl.when(has_far)
     def _():
-        for there in (ahead, behind):
-            pl.semaphore_signal(barrier, inc=1, device_id=there, device_id_type=MESH)
-
-        @pl.when(y == ny - 1)
-        def _():
-            pl.semaphore_signal(barrier, inc=1, device_id=up, device_id_type=MESH)
-
-        @pl.when(y == 0)
-        def _():
-            pl.semaphore_signal(barrier, inc=1, device_id=down, device_id_type=MESH)
+        pl.semaphore_signal(barrier, inc=1, device_id=across, device_id_type=MESH)
 
     for dy, dz, there, exists in around:
         @pl.when(exists)
@@ -234,8 +220,7 @@
 
     rows_near = 3 - jnp.where(y == 0, 1, 0) - jnp.where(y == ny - 1, 1, 0)
     columns_near = 3 - jnp.where(z == 0, 1, 0) - jnp.where(z == nz - 1, 1, 0)
-    ring_peers = 2 + jnp.where(y == 0, 1, 0) + jnp.where(y == ny - 1, 1, 0)
-    pl.semaphore_wait(barrier, rows_near * columns_near + jnp.where(has_far, ring_peers, 0))
+    pl.semaphore_wait(barrier, rows_near * columns_near + jnp.where(has_far, 1, 0))
 
     def send_tiles(feat_from, pos_from, feat_to, pos_to, k, there):
         return (
@@ -250,14 +235,6 @@
     def send_rows(source, target, k, there):
         return send_tiles(near_feat.at[source], near_pos.at[source], near_feat.at[target], near_pos.at[target], k, there)
 
-    def start(copies):
-        for copy in copies:
-            copy.start()
-
-    def arrive(copies):
-        for copy in copies:
-            copy.wait_recv()
-
     def leave(copies):
         for copy in copies:
             copy.wait_send()
@@ -273,70 +250,73 @@
             far_sends[t].append(send_rows(pl.ds((far_base + 4) * T + t, 1), target, 8 + 8 * t + k, there))
         pair_sends.append(send_rows(cells(9 + cell_of(dy, dz)), cells(far_base + cell_of(dy, dz)), 24 + k, partner))
     centre_send = send_rows(cells(13), cells(far_base + 4), 32, partner)
-    hops, relays = [], []
-    for t, (first, last, last_base) in enumerate(((up, ahead, ahead_base), (down, behind, behind_base))):
-        slot, source = pl.ds(t, 1), pl.ds(13 * T + t, 1)
-        hops.append(
-            send_tiles(near_feat.at[source], near_pos.at[source], relay_feat.at[slot], relay_pos.at[slot], 33 + t, first)
-        )
-        target = pl.ds((last_base + 4) * T + t, 1)
-        relays.append(
-            send_tiles(relay_feat.at[slot], relay_pos.at[slot], near_feat.at[target], near_pos.at[target], 35 + t, last)
-        )
-
-    @pl.when(has_far)
-    def _():
-        for t in range(T):
-            start(hops[t])
-        for t in range(T):
-            arrive(hops[t])
-            start(relays[t])
-
-    for k in range(8):
-        @pl.when(around[k][3])
-        def _():
-            start(own_sends[k])
-
-    start(centre_send)
-    for k in range(8):
-        @pl.when(around[k][3])
-        def _():
-            arrive(own_sends[7 - k])
-            start(pair_sends[k])
-
-    for k in range(8):
-        @pl.when(around[k][3])
-        def _():
-            arrive(pair_sends[k])
-
-    arrive(centre_send)
-
-    @pl.when(has_far)
-    def _():
-        for t in range(T):
-            arrive(relays[t])
-            for k in range(8):
-                @pl.when(around[k][3])
-                def _():
-                    start(far_sends[t][k])
-        for t in range(T):
-            for k in range(8):
-                @pl.when(around[k][3])
-                def _():
-                    arrive(far_sends[t][7 - k])
+    crossing = [
+        send_rows(pl.ds(13 * T + t, 1), pl.ds((pair_base + 4) * T + t, 1), 33 + t, across) for t in range(T)
+    ]
+
+    for kind in (1, 0):
+        @pl.when(has_far)
+        def _():
+            for t in range(T):
+                crossing[t][kind].start()
+
+        for k in range(8):
+            @pl.when(around[k][3])
+            def _():
+                own_sends[k][kind].start()
+
+        centre_send[kind].start()
+
+    for kind in (1, 0):
+        for k in range(8):
+            @pl.when(around[k][3])
+            def _():
+                own_sends[7 - k][kind].wait_recv()
+                pair_sends[k][kind].start()
+
+    def receive(kind):
+        @pl.when(has_far)
+        def _():
+            for t in range(T):
+                crossing[t][kind].wait_recv()
+                for k in range(8):
+                    @pl.when(around[k][3])
+                    def _():
+                        far_sends[t][k][kind].start()
+
+        for k in range(8):
+            @pl.when(around[k][3])
+            def _():
+                pair_sends[k][kind].wait_recv()
+
+        centre_send[kind].wait_recv()
+
+        @pl.when(has_far)
+        def _():
+            for t in range(T):
+                for k in range(8):
+                    @pl.when(around[k][3])
+                    def _():
+                        far_sends[t][7 - k][kind].wait_recv()
+
+    receive(1)
+
+    def expand(t, carry):
+        tile_basis(t, nbr, rates, pos, near_pos, own, basis)
+        return carry
+
+    lax.fori_loop(0, T, expand, 0)
+    receive(0)
 
     def gradients(t, carry):
-        tile_gradients(
-            t, nbr, counts, rates, pos, near_pos, near_feat, mix, readout,
-            own, basis, stack, sums, inv, grad, contrib,
-        )
+        tile_gradients(t, nbr, counts, near_feat, mix, readout, basis, stack, sums, inv, grad, contrib)
         return carry
 
     lax.fori_loop(0, T, gradients, 0)
 
     folds = [
-        Fold(refs, source, inverse, around, (up, down), (ahead, behind), partner, (x, y, z), (ny, nz), (pair_base, far_base))
-        for refs, source in ((fold_refs[:13], contrib), (fold_refs[13:], contrib_force))
+        Fold(refs, source, inverse, around, across, partner, (x, y, z), (ny, nz), (pair_base, far_base))
+        for refs, source in ((fold_refs[:16], contrib), (fold_refs[16:], contrib_force))
     ]
     feature, push = folds
 
@@ -358,7 +338,6 @@
 
     @pl.when(has_far)
     def _():
-        feature.relay()
         push.send_far_column()
 
     push.send_pair_column()
@@ -369,10 +348,6 @@
         push.sum_far_column()
 
     push.send_sides()
-
-    @pl.when(has_far)
-    def _():
-        push.relay()
 
     feature.send_rows()
     push.send_rows()
@@ -392,8 +367,7 @@
     @pl.when(has_far)
     def _():
         for t in range(T):
-            leave(hops[t])
-            leave(relays[t])
+            leave(crossing[t])
         for k in range(8):
             @pl.when(around[k][3])
             def _():
@@ -412,10 +386,10 @@
 
 
 class Fold:
-    def __init__(self, refs, source, inverse, around, near_ring, far_ring, partner, me, sizes, bases):
+    def __init__(self, refs, source, inverse, around, across, partner, me, sizes, bases):
         (
-            self.far_out, self.far_in, self.far_sum, self.passing, self.far_got,
-            self.pair_out, self.pair_in, self.side_out, self.side_in, self.mid, self.row_in, send, recv,
+            self.far_out, self.far_in, self.far_sum, self.far_got,
+            self.pair_out, self.pair_in, self.side_out, self.side_in, self.mid, self.row_in, send, recv, *self.coded
         ) = refs
         self.source, self.inverse, self.around = source, inverse, around
         self.pair_base, self.far_base = bases
@@ -432,8 +406,11 @@
         self.side_exists = [z > 0, z < nz - 1]
         self.row = [copy(self.mid.at[2 * d], self.row_in.at[d], 11 + d, (x, y + 2 * d - 1, z)) for d in range(2)]
         self.row_exists = [y > 0, y < ny - 1]
-        self.hop = [copy(self.far_sum.at[t], self.passing.at[t], 13 + t, near_ring[t]) for t in range(T)]
-        self.last = [copy(self.passing.at[t], self.far_got.at[t], 15 + t, far_ring[t]) for t in range(T)]
+        if self.coded:
+            code_out, code_in, step_out, step_in = self.coded
+            self.cross = [copy(step_out, step_in, 13, across), copy(code_out, code_in, 14, across)]
+        else:
+            self.cross = [copy(self.far_sum, self.far_got, 13, across)]
 
     def fill(self, ref, cell, extra=None):
         def one(u, carry):
@@ -471,13 +448,19 @@
             def _():
                 self.far[7 - k].wait_recv()
                 self.far_sum[...] += self.far_in[7 - k]
+        if self.coded:
+            self.encode()
+        for part in self.cross:
+            part.start()
+
+    def encode(self):
+        code_out, _, step_out, _ = self.coded
         for t in range(T):
-            self.hop[t].start()
-
-    def relay(self):
-        for t in range(T):
-            self.hop[t].wait_recv()
-            self.last[t].start()
+            block = self.far_sum[t]
+            largest = jnp.maximum(jnp.max(jnp.abs(block), axis=0, keepdims=True), 1e-30)
+            step_out[t] = jnp.broadcast_to(largest * (1.0 / 32767.0), (8, C))
+            code = (block * (32767.0 / largest) + 32768.5).astype(jnp.int32) - 32768
+            code_out[t] = code.astype(jnp.int16)
 
     def send_sides(self):
         self.pair.wait_recv()
@@ -512,9 +495,15 @@
                 self.mid[1] += self.row_in[1 - d]
 
     def finish_far(self):
+        for part in self.cross:
+            part.wait_recv()
         for t in range(T):
-            self.last[t].wait_recv()
-            self.mid[1, t] += self.far_got[t]
+            if self.coded:
+                _, code_in, _, step_in = self.coded
+                got = code_in[t].astype(jnp.int32).astype(jnp.float32) * step_in[t, 0:1, :]
+            else:
+                got = self.far_got[t]
+            self.mid[1, t] += got
 
     def leave(self, has_far):
         @pl.when(has_far)
@@ -523,9 +512,8 @@
                 @pl.when(self.around[k][3])
                 def _():
                     self.far[k].wait_send()
-            for t in range(T):
-                self.hop[t].wait_send()
-                self.last[t].wait_send()
+            for part in self.cross:
+                part.wait_send()
 
         self.pair.wait_send()
         for d in range(2):
@@ -539,8 +527,8 @@
 
 
 def fold_scratch(tile):
-    shapes = [(8, T), (8, T), (T,), (T,), (T,), (9, T), (9, T), (2, 3, T), (2, 3, T), (3, T), (2, T)]
-    return [pltpu.VMEM((*lead, *tile), jnp.float32) for lead in shapes] + [pltpu.SemaphoreType.DMA((17,))] * 2
+    shapes = [(8, T), (8, T), (T,), (T,), (9, T), (9, T), (2, 3, T), (2, 3, T), (3, T), (2, T)]
+    return [pltpu.VMEM((*lead, *tile), jnp.float32) for lead in shapes] + [pltpu.SemaphoreType.DMA((15,))] * 2
 
 
 def body(positions, features, counts, neighbours, mix_weight, readout, radial_rates):
@@ -558,8 +546,6 @@
             pltpu.SMEM((T * NEAR,), jnp.int32),
             pltpu.VMEM((NEAR, A, C), jnp.bfloat16),
             pltpu.VMEM((NEAR, 3, A), jnp.float32),
-            pltpu.VMEM((T, A, C), jnp.bfloat16),
-            pltpu.VMEM((T, 3, A), jnp.float32),
             pltpu.VMEM((T, 3, A, A), jnp.float32),
             pltpu.VMEM((T, 4 * R * A, S * A), jnp.bfloat16),
             pltpu.VMEM((T, S * A, C), jnp.bfloat16),
@@ -571,11 +557,15 @@
             pltpu.VMEM((T, 3, A), jnp.float32),
             pltpu.VMEM((T * S, A, C), jnp.float32),
             pltpu.VMEM((T * S, 8, A), jnp.float32),
-            pltpu.SemaphoreType.DMA((37,)),
-            pltpu.SemaphoreType.DMA((37,)),
-            pltpu.SemaphoreType.DMA((37,)),
-            pltpu.SemaphoreType.DMA((37,)),
+            pltpu.SemaphoreType.DMA((35,)),
+            pltpu.SemaphoreType.DMA((35,)),
+            pltpu.SemaphoreType.DMA((35,)),
+            pltpu.SemaphoreType.DMA((35,)),
             *fold_scratch((A, C)),
+            pltpu.VMEM((T, A, C), jnp.int16),
+            pltpu.VMEM((T, A, C), jnp.int16),
+            pltpu.VMEM((T, 8, C), jnp.float32),
+            pltpu.VMEM((T, 8, C), jnp.float32),
             *fold_scratch((8, A)),
         ],
         compiler_params=pltpu.CompilerParams(

time: 115 us -> 103 us (0.90); the launches traced: 113 us -> 103 us
  Pallas kernels: 108 us -> 97.6 us
    pallas_call x1, Pallas kernels: 108 us -> 97.6 us  [body(): pl.pallas_call(step_kernel, out_shape=(jax.ShapeDtypeStruct((T, 3, A), jn...]
where the time goes in v4:
time: 103 us
  Pallas kernels  97.6 us (95%)
  local copies, waits for them, and re-layouts  4.66 us (5%)
    pallas_call x1, Pallas kernels, body(): pl.pallas_call(step_kernel, out_shape=(jax.ShapeDtypeStruct((T, 3, A), jn...  97.6 us
    unnamed x9, local copies, waits for them, and re-layouts  4.07 us

profile of v4, /device:TPU:25, one launch (start us, length us, event | category | flops | bytes accessed | tf_op | source)
XLA Modules:
  0.0 103.0 jit_solution(8276911309171691041)
XLA Ops:
  0.6 0.0 copy-start.2
  0.6 0.0 copy-start.1
  0.6 0.7 copy-done.2
  1.3 0.6 reshape.25.nbr
  1.9 0.0 copy-done.1
  1.9 0.6 copy.12
  2.5 97.6 %shard_map.86 = (f32[2,3,128]{2,1,0:T(4,128)}, f32[2,128,128]{2,1,0:T(8,128)}) custom-call(s32[16]{0:T(128)} %reshape.25.nbr, s32[2]{0:T(128)} %bitcast.12, f32[4]{0:T(128)} %rates.1, f32[2,3,128]{2,1,0:T(4,128)} %bitcast.10, bf16[2,128,128]{2,1,0:T(8,128)(2,1)} %bitcast.9, bf16[1024,128]{1,0:T(8,128)(2,1)} %mix.1, f32[1,128]{1,0:T(1,128)} %bitcast.13), custom_call_target="tpu_custom_call" | custom-call | tf_op jit(solution)/shard_map/pallas_call | solution.py:537
  100.1 0.0 copy-start
  100.1 0.7 copy-done
  100.8 0.6 copy.10
  101.4 1.6 %copy.14 = f32[1,1,1,2,128,128]{5,4,3,2,1,0:T(8,128)} copy(f32[1,1,1,2,128,128]{5,4,3,2,1,0:T(8,128)} %bitcast.8) | data formatting | bytes 262144
Async XLA Ops:
  0.6 0.7 copy-start.2
  0.6 1.3 %copy-start.1 = (f32[1,1,1,2,3,128]{5,3,4,2,1,0:T(2,128)S(1)}, f32[1,1,1,2,3,128]{5,3,4,2,1,0:T(2,128)}, u32[]{:S(2)}) copy-start(f32[1,1,1,2,3,128]{5,3,4,2,1,0:T(2,128)} %param.7) | copy-start | bytes 9220
  100.1 0.7 copy-start
